TPU v7x, 128 devices: a whole 4x4x4 slice. The times are simulated.
128 devices in a mesh: data: 64 (over z, y, x), stage: 2 (over core).
Axes of the slice: x: 4, y: 4, z: 4, core: 2. Of those that a mesh axis runs over, the one named last changes fastest.
Arguments:
- x: bfloat16 [8, 128, 32, 1024], P(None, 'data')
- g: bfloat16 [8, 128, 32, 1024], P(None, 'data')
- w_gate: bfloat16 [2, 1, 1024, 4096], P('stage', None, 'data')
- w_in: bfloat16 [2, 1, 1024, 4096], P('stage', None, 'data')
- w_out: bfloat16 [2, 1, 4096, 1024], P('stage', None, 'data')
Outputs:
- output 1: bfloat16 [8, 128, 32, 1024], P(None, 'data')
- output 2: float32 [2, 1, 1024, 4096], P('stage', None, 'data')
- output 3: float32 [2, 1, 1024, 4096], P('stage', None, 'data')
- output 4: float32 [2, 1, 4096, 1024], P('stage', None, 'data')
All inputs are finite; a program needn't handle non-finite values.
Results may differ from a plain program's by a relative error of at most 0.0116991.
Values are sent between devices in bfloat16 or wider.
A program may use at most 1 GiB of HBM per device.

v0:
```python
import jax
import jax.numpy as jnp
from jax import lax
from jax.sharding import PartitionSpec as P


def rms_f32(row_vals):
    return row_vals * lax.rsqrt(jnp.mean(row_vals * row_vals, axis=-1, keepdims=True) + 1e-6)


def layer_fwd(tokens, w_gate, w_in, w_out):
    normed = rms_f32(tokens.astype(jnp.float32)).astype(jnp.bfloat16)
    pre_gate = jnp.dot(normed, w_gate, preferred_element_type=jnp.float32)
    pre_in = jnp.dot(normed, w_in, preferred_element_type=jnp.float32)
    hidden = (pre_gate * jax.nn.sigmoid(pre_gate) * pre_in).astype(jnp.bfloat16)
    branch = jnp.dot(hidden, w_out, preferred_element_type=jnp.float32)
    return tokens + branch.astype(jnp.bfloat16)


def layer_bwd(tokens, d_next, w_gate, w_in, w_out):
    normed_f, rms_pull = jax.vjp(rms_f32, tokens.astype(jnp.float32))
    normed = normed_f.astype(jnp.bfloat16)
    pre_gate = jnp.dot(normed, w_gate, preferred_element_type=jnp.float32)
    pre_in = jnp.dot(normed, w_in, preferred_element_type=jnp.float32)
    sigma_gate = jax.nn.sigmoid(pre_gate)
    gate_act = pre_gate * sigma_gate
    hidden = (gate_act * pre_in).astype(jnp.bfloat16)
    d_wout = jnp.einsum('tf,td->fd', hidden, d_next, preferred_element_type=jnp.float32)
    d_hidden = jnp.einsum('td,fd->tf', d_next, w_out, preferred_element_type=jnp.float32)
    d_gate = (d_hidden * pre_in * sigma_gate * (1.0 + pre_gate * (1.0 - sigma_gate))).astype(jnp.bfloat16)
    d_up = (d_hidden * gate_act).astype(jnp.bfloat16)
    d_wgate = jnp.einsum('td,tf->df', normed, d_gate, preferred_element_type=jnp.float32)
    d_win = jnp.einsum('td,tf->df', normed, d_up, preferred_element_type=jnp.float32)
    d_normed = jnp.einsum('tf,df->td', d_gate, w_gate, preferred_element_type=jnp.float32) + jnp.einsum('tf,df->td', d_up, w_in, preferred_element_type=jnp.float32)
    d_resid = rms_pull(d_normed)[0]
    d_prev = (d_next.astype(jnp.float32) + d_resid).astype(jnp.bfloat16)
    return d_prev, d_wgate, d_win, d_wout


def solution(mesh):
    stages = mesh.shape['stage']
    act_spec = P(None, 'data', None, None)
    weight_spec = P('stage', None, 'data', None)
    fwd_pairs = [(source_id, source_id + 1) for source_id in range(stages - 1)]
    bwd_pairs = [(source_id + 1, source_id) for source_id in range(stages - 1)]

    def per_device(x, g, w_gate, w_in, w_out):
        n_micro, batch_mb, seq_len, dmodel = x.shape
        layers = w_gate.shape[1]
        ffn_dim = w_gate.shape[3]
        row_count = batch_mb * seq_len
        stage_idx = lax.axis_index('stage')
        x_micro = x.reshape(n_micro, row_count, dmodel)
        g_micro = g.reshape(n_micro, row_count, dmodel)
        n_ticks = n_micro + stages - 1

        gate_full = lax.all_gather(w_gate[0], 'data', axis=1, tiled=True)
        in_full = lax.all_gather(w_in[0], 'data', axis=1, tiled=True)
        out_full = lax.all_gather(w_out[0], 'data', axis=1, tiled=True)

        def fwd_tick(loop_state, tick_id):
            received, saved_in = loop_state
            micro_id = tick_id - stage_idx
            is_valid = (micro_id >= 0) & (micro_id < n_micro)
            micro_slot = jnp.clip(micro_id, 0, n_micro - 1)
            fresh_in = lax.dynamic_index_in_dim(x_micro, micro_slot, 0, keepdims=False)
            block_in = jnp.where(stage_idx == 0, fresh_in, received)

            def run_stage(operands):
                tokens, stored_in = operands
                layer_inputs = []
                for layer_id in range(layers):
                    layer_inputs.append(tokens)
                    tokens = layer_fwd(tokens, gate_full[layer_id], in_full[layer_id], out_full[layer_id])
                stored_in = lax.dynamic_update_index_in_dim(stored_in, jnp.stack(layer_inputs), micro_slot, 0)
                return tokens, stored_in

            def skip_stage(operands):
                return operands

            block_out, saved_in = lax.cond(is_valid, run_stage, skip_stage, (block_in, saved_in))
            sent_out = lax.ppermute(block_out, 'stage', fwd_pairs)
            return (sent_out, saved_in), None

        saved_init = jnp.zeros((n_micro, layers, row_count, dmodel), jnp.bfloat16)
        recv_init = jnp.zeros((row_count, dmodel), jnp.bfloat16)
        (_, saved_in), _ = lax.scan(fwd_tick, (recv_init, saved_init), jnp.arange(n_ticks))

        gate_shard, in_shard, out_shard, saved_in = lax.optimization_barrier((w_gate[0], w_in[0], w_out[0], saved_in))
        gate_back = lax.all_gather(gate_shard, 'data', axis=1, tiled=True)
        in_back = lax.all_gather(in_shard, 'data', axis=1, tiled=True)
        out_back = lax.all_gather(out_shard, 'data', axis=1, tiled=True)

        def bwd_tick(loop_state, tick_id):
            received, grad_sums, dx_buf = loop_state
            micro_id = tick_id - (stages - 1 - stage_idx)
            is_valid = (micro_id >= 0) & (micro_id < n_micro)
            micro_slot = jnp.clip(micro_id, 0, n_micro - 1)
            fresh_in = lax.dynamic_index_in_dim(g_micro, micro_slot, 0, keepdims=False)
            d_out = jnp.where(stage_idx == stages - 1, fresh_in, received)

            def run_stage(operands):
                d_cur, old_sums, dx_store = operands
                layer_inputs = lax.dynamic_index_in_dim(saved_in, micro_slot, 0, keepdims=False)
                gate_sums = list(old_sums[0])
                in_sums = list(old_sums[1])
                out_sums = list(old_sums[2])
                for layer_id in reversed(range(layers)):
                    d_cur, d_wgate, d_win, d_wout = layer_bwd(layer_inputs[layer_id], d_cur, gate_back[layer_id], in_back[layer_id], out_back[layer_id])
                    gate_sums[layer_id] = gate_sums[layer_id] + d_wgate
                    in_sums[layer_id] = in_sums[layer_id] + d_win
                    out_sums[layer_id] = out_sums[layer_id] + d_wout
                dx_store = lax.dynamic_update_index_in_dim(dx_store, d_cur, micro_slot, 0)
                return d_cur, (tuple(gate_sums), tuple(in_sums), tuple(out_sums)), dx_store

            def skip_stage(operands):
                return operands

            d_in, grad_sums, dx_buf = lax.cond(is_valid, run_stage, skip_stage, (d_out, grad_sums, dx_buf))
            sent_out = lax.ppermute(d_in, 'stage', bwd_pairs)
            return (sent_out, grad_sums, dx_buf), None

        zero_up = jnp.zeros((dmodel, ffn_dim), jnp.float32)
        zero_down = jnp.zeros((ffn_dim, dmodel), jnp.float32)
        grad_init = (tuple(zero_up for _ in range(layers)), tuple(zero_up for _ in range(layers)), tuple(zero_down for _ in range(layers)))
        dx_init = jnp.zeros((n_micro, row_count, dmodel), jnp.bfloat16)
        (_, grad_sums, dx_buf), _ = lax.scan(bwd_tick, (recv_init, grad_init, dx_init), jnp.arange(n_ticks))

        gate_grad = lax.psum_scatter(jnp.stack(grad_sums[0]), 'data', scatter_dimension=1, tiled=True)
        in_grad = lax.psum_scatter(jnp.stack(grad_sums[1]), 'data', scatter_dimension=1, tiled=True)
        out_grad = lax.psum_scatter(jnp.stack(grad_sums[2]), 'data', scatter_dimension=1, tiled=True)
        dx_own = jnp.where(stage_idx == 0, dx_buf, jnp.zeros_like(dx_buf))
        d_x = lax.psum(dx_own, 'stage').reshape(x.shape)
        return d_x, gate_grad[None], in_grad[None], out_grad[None]

    return jax.shard_map(per_device, mesh=mesh, in_specs=(act_spec, act_spec, weight_spec, weight_spec, weight_spec), out_specs=(act_spec, weight_spec, weight_spec, weight_spec), check_vma=False)
```

profile of v0, /device:TPU:0, one launch (start us, length us, event | category | flops | bytes accessed | tf_op | source)
XLA Modules:
  0.0 2510.9 jit_solution(3539204646434192405)
XLA Ops:
  9.4 82.0 %all-gather.16.cloned.1.call-done = bf16[1,1,1024,4096]{3,2,1,0:T(8,128)(2,1)} async-done(((bf16[1,1,16,4096]{3,2,1,0:T(8,128)(2,1)}), bf16[1,1,1024,4096]{3,2,1,0:T(8,128)(2,1)}) %all-gather.16.cloned.1.call-update) | async-done | bytes 8388624 | tf_op jit(solution)/shard_map/all_gather | solution.py:57
  91.4 80.5 %all-gather.18.cloned.1.call-done = bf16[1,1,1024,4096]{3,2,1,0:T(8,128)(2,1)} async-done(((bf16[1,1,16,4096]{3,2,1,0:T(8,128)(2,1)}), bf16[1,1,1024,4096]{3,2,1,0:T(8,128)(2,1)}) %all-gather.18.cloned.1.call-update) | async-done | bytes 8388624 | tf_op jit(solution)/shard_map/all_gather | solution.py:58
  172.0 80.5 %all-gather.20.cloned.1.call-done = bf16[1,1,4096,1024]{3,2,1,0:T(8,128)(2,1)} async-done(((bf16[1,1,64,1024]{3,2,1,0:T(8,128)(2,1)}), bf16[1,1,4096,1024]{3,2,1,0:T(8,128)(2,1)}) %all-gather.20.cloned.1.call-update) | async-done | bytes 8388624 | tf_op jit(solution)/shard_map/all_gather | solution.py:59
  253.6 180.2 %while.33 = (s32[]{:T(128)}, bf16[64,1024]{1,0:T(8,128)(2,1)S(1)}, bf16[8,1,64,1024]{3,2,1,0:T(8,128)(2,1)}, s32[9]{0:T(128)S(1)}, s32[]{:T(128)}, /*index=5*/pr...) while((s32[]{:T(128)}, bf16[64,1024]{1,0:T(8,128)(2,1)S(1)}, ...), condition=%wide.region_4.5_spmd, body=%wide.region_0.4_spmd.sunk | while | flops 1613168640 | bytes 28968560 | solution.py:87
  255.8 14.7 conditional.4
  261.0 8.9 fusion.15
  274.9 14.7 conditional.4
  280.1 8.9 fusion.15
  295.1 14.7 conditional.4
  300.2 8.9 fusion.15
  315.2 14.7 conditional.4
  320.4 8.9 fusion.15
  335.3 14.7 conditional.4
  340.5 8.9 fusion.15
  355.4 14.7 conditional.4
  360.6 8.9 fusion.15
  375.6 14.7 conditional.4
  380.7 8.9 fusion.15
  395.7 14.7 conditional.4
  400.9 8.9 fusion.15
  415.9 16.9 collective-permute-start
  435.0 76.6 %all-gather.10.cloned.1.call-done = bf16[1,4096,1024]{2,1,0:T(8,128)(2,1)} async-done(((bf16[1,64,1024]{2,1,0:T(8,128)(2,1)}), bf16[1,4096,1024]{2,1,0:T(8,128)(2,1)}) %all-gather.10.cloned.1.call-update) | async-done | bytes 8388624 | tf_op jit(solution)/shard_map/all_gather | solution.py:92
  511.6 80.4 %all-gather.12.cloned.1.call-done = bf16[1,1024,4096]{2,1,0:T(8,128)(2,1)} async-done(((bf16[1,16,4096]{2,1,0:T(8,128)(2,1)}), bf16[1,1024,4096]{2,1,0:T(8,128)(2,1)}) %all-gather.12.cloned.1.call-update) | async-done | bytes 8388624 | tf_op jit(solution)/shard_map/all_gather | solution.py:91
  591.9 80.4 %all-gather.14.cloned.1.call-done = bf16[1,1024,4096]{2,1,0:T(8,128)(2,1)} async-done(((bf16[1,16,4096]{2,1,0:T(8,128)(2,1)}), bf16[1,1024,4096]{2,1,0:T(8,128)(2,1)}) %all-gather.14.cloned.1.call-update) | async-done | bytes 8388624 | tf_op jit(solution)/shard_map/all_gather | solution.py:90
  672.5 7.9 broadcast_in_dim.35.clone
  680.3 7.9 broadcast_in_dim.36
  688.2 7.9 broadcast_in_dim.35
  696.1 608.2 %while.34 = (s32[]{:T(128)}, bf16[64,1024]{1,0:T(8,128)(2,1)S(1)}, f32[1024,4096]{1,0:T(8,128)}, f32[1024,4096]{1,0:T(8,128)}, f32[4096,1024]{1,0:T(8,128)}, /*i...) while((s32[]{:T(128)}, bf16[64,1024]{1,0:T(8,128)(2,1)S(1)}, ...), condition=%wide.region_10.11_spmd, body=%wide.region_5.10_spmd.sunk | while | flops 4314366464 | bytes 331747328 | solution.py:127
  699.6 62.6 %collective-permute-done.1 = bf16[64,1024]{1,0:T(8,128)(2,1)S(1)} collective-permute-done((bf16[64,1024]{1,0:T(8,128)(2,1)S(1)}, bf16[64,1024]{1,0:T(8,128)(2,1)S(1)}, u32[]{:S(2)}, u32[]{:S(2)}) %collective-permute-start.1) | collective-permute-done | bytes 131104 | tf_op jit(solution)/shard_map/while/body/eval_jaxpr/ppermute | solution.py:120
  764.5 62.3 %conditional.5 = (bf16[64,1024]{1,0:T(8,128)(2,1)S(1)}, f32[1024,4096]{1,0:T(8,128)}, f32[1024,4096]{1,0:T(8,128)}, f32[4096,1024]{1,0:T(8,128)}, bf16[8,64,1024]{2,1,0:T(8,128)(2,1)S(1)}) conditional(s32[]{:T(128)} %convert_element_type.125, (bf16[64,1024]{1,0:T(8,128)(2,1)S(1)}, f32[1024,4096]{1,0:T(8,128)}, f32[1024,4096]{1,0:T(8,128)}, ...), branch_computations={%region_6.6_spmd, %region_7.9_spmd} | conditional | flops 4314300928 | bytes 330829440 | solution.py:119
  774.1 6.2 multiply_convert_fusion.1
  788.5 14.1 convolution_add_fusion
  806.7 20.1 convolution_add_fusion.2
  832.2 62.3 %conditional.5 = (bf16[64,1024]{1,0:T(8,128)(2,1)S(1)}, f32[1024,4096]{1,0:T(8,128)}, f32[1024,4096]{1,0:T(8,128)}, f32[4096,1024]{1,0:T(8,128)}, bf16[8,64,1024]{2,1,0:T(8,128)(2,1)S(1)}) conditional(s32[]{:T(128)} %convert_element_type.125, (bf16[64,1024]{1,0:T(8,128)(2,1)S(1)}, f32[1024,4096]{1,0:T(8,128)}, f32[1024,4096]{1,0:T(8,128)}, ...), branch_computations={%region_6.6_spmd, %region_7.9_spmd} | conditional | flops 4314300928 | bytes 330829440 | solution.py:119
  841.8 6.2 multiply_convert_fusion.1
  856.3 14.1 convolution_add_fusion
  874.4 20.1 convolution_add_fusion.2
  900.0 62.3 %conditional.5 = (bf16[64,1024]{1,0:T(8,128)(2,1)S(1)}, f32[1024,4096]{1,0:T(8,128)}, f32[1024,4096]{1,0:T(8,128)}, f32[4096,1024]{1,0:T(8,128)}, bf16[8,64,1024]{2,1,0:T(8,128)(2,1)S(1)}) conditional(s32[]{:T(128)} %convert_element_type.125, (bf16[64,1024]{1,0:T(8,128)(2,1)S(1)}, f32[1024,4096]{1,0:T(8,128)}, f32[1024,4096]{1,0:T(8,128)}, ...), branch_computations={%region_6.6_spmd, %region_7.9_spmd} | conditional | flops 4314300928 | bytes 330829440 | solution.py:119
  909.6 6.2 multiply_convert_fusion.1
  924.0 14.1 convolution_add_fusion
  942.2 20.1 convolution_add_fusion.2
  967.7 62.3 %conditional.5 = (bf16[64,1024]{1,0:T(8,128)(2,1)S(1)}, f32[1024,4096]{1,0:T(8,128)}, f32[1024,4096]{1,0:T(8,128)}, f32[4096,1024]{1,0:T(8,128)}, bf16[8,64,1024]{2,1,0:T(8,128)(2,1)S(1)}) conditional(s32[]{:T(128)} %convert_element_type.125, (bf16[64,1024]{1,0:T(8,128)(2,1)S(1)}, f32[1024,4096]{1,0:T(8,128)}, f32[1024,4096]{1,0:T(8,128)}, ...), branch_computations={%region_6.6_spmd, %region_7.9_spmd} | conditional | flops 4314300928 | bytes 330829440 | solution.py:119
  977.3 6.2 multiply_convert_fusion.1
  991.8 14.1 convolution_add_fusion
  1009.9 20.1 convolution_add_fusion.2
  1035.5 62.3 %conditional.5 = (bf16[64,1024]{1,0:T(8,128)(2,1)S(1)}, f32[1024,4096]{1,0:T(8,128)}, f32[1024,4096]{1,0:T(8,128)}, f32[4096,1024]{1,0:T(8,128)}, bf16[8,64,1024]{2,1,0:T(8,128)(2,1)S(1)}) conditional(s32[]{:T(128)} %convert_element_type.125, (bf16[64,1024]{1,0:T(8,128)(2,1)S(1)}, f32[1024,4096]{1,0:T(8,128)}, f32[1024,4096]{1,0:T(8,128)}, ...), branch_computations={%region_6.6_spmd, %region_7.9_spmd} | conditional | flops 4314300928 | bytes 330829440 | solution.py:119
  1045.1 6.2 multiply_convert_fusion.1
  1059.5 14.1 convolution_add_fusion
  1077.7 20.1 convolution_add_fusion.2
  1103.3 62.3 %conditional.5 = (bf16[64,1024]{1,0:T(8,128)(2,1)S(1)}, f32[1024,4096]{1,0:T(8,128)}, f32[1024,4096]{1,0:T(8,128)}, f32[4096,1024]{1,0:T(8,128)}, bf16[8,64,1024]{2,1,0:T(8,128)(2,1)S(1)}) conditional(s32[]{:T(128)} %convert_element_type.125, (bf16[64,1024]{1,0:T(8,128)(2,1)S(1)}, f32[1024,4096]{1,0:T(8,128)}, f32[1024,4096]{1,0:T(8,128)}, ...), branch_computations={%region_6.6_spmd, %region_7.9_spmd} | conditional | flops 4314300928 | bytes 330829440 | solution.py:119
  1127.3 14.1 convolution_add_fusion
  1145.4 20.1 convolution_add_fusion.2
  1171.0 62.3 %conditional.5 = (bf16[64,1024]{1,0:T(8,128)(2,1)S(1)}, f32[1024,4096]{1,0:T(8,128)}, f32[1024,4096]{1,0:T(8,128)}, f32[4096,1024]{1,0:T(8,128)}, bf16[8,64,1024]{2,1,0:T(8,128)(2,1)S(1)}) conditional(s32[]{:T(128)} %convert_element_type.125, (bf16[64,1024]{1,0:T(8,128)(2,1)S(1)}, f32[1024,4096]{1,0:T(8,128)}, f32[1024,4096]{1,0:T(8,128)}, ...), branch_computations={%region_6.6_spmd, %region_7.9_spmd} | conditional | flops 4314300928 | bytes 330829440 | solution.py:119
  1180.6 6.2 multiply_convert_fusion.1
  1195.0 14.1 convolution_add_fusion
  1213.2 20.1 convolution_add_fusion.2
  1238.7 62.3 %conditional.5 = (bf16[64,1024]{1,0:T(8,128)(2,1)S(1)}, f32[1024,4096]{1,0:T(8,128)}, f32[1024,4096]{1,0:T(8,128)}, f32[4096,1024]{1,0:T(8,128)}, bf16[8,64,1024]{2,1,0:T(8,128)(2,1)S(1)}) conditional(s32[]{:T(128)} %convert_element_type.125, (bf16[64,1024]{1,0:T(8,128)(2,1)S(1)}, f32[1024,4096]{1,0:T(8,128)}, f32[1024,4096]{1,0:T(8,128)}, ...), branch_computations={%region_6.6_spmd, %region_7.9_spmd} | conditional | flops 4314300928 | bytes 330829440 | solution.py:119
  1248.3 6.2 multiply_convert_fusion.1
  1262.8 14.1 convolution_add_fusion
  1280.9 20.1 convolution_add_fusion.2
  1307.4 22.2 all-reduce.2.cloned.1.call-done
  1329.7 393.9 %reduce-scatter.8.cloned.1.call-done = f32[1,64,1024]{2,1,0:T(8,128)} async-done(((f32[1,4096,1024]{2,1,0:T(8,128)}), f32[1,64,1024]{2,1,0:T(8,128)}) %reduce-scatter.8.cloned.1.call-update) | async-done | bytes 262160 | tf_op jit(solution)/shard_map/reduce_scatter | solution.py:131
  1723.6 390.2 %reduce-scatter.4.cloned.1.call-done = f32[1,16,4096]{2,1,0:T(8,128)} async-done(((f32[1,1024,4096]{2,1,0:T(8,128)}), f32[1,16,4096]{2,1,0:T(8,128)}) %reduce-scatter.4.cloned.1.call-update) | async-done | bytes 262160 | tf_op jit(solution)/shard_map/reduce_scatter | solution.py:129
  2113.8 388.0 %reduce-scatter.6.cloned.1.call-done = f32[1,16,4096]{2,1,0:T(8,128)} async-done(((f32[1,1024,4096]{2,1,0:T(8,128)}), f32[1,16,4096]{2,1,0:T(8,128)}) %reduce-scatter.6.cloned.1.call-update) | async-done | bytes 262160 | tf_op jit(solution)/shard_map/reduce_scatter | solution.py:130
  (407 shorter events, 316.9 us)
Async XLA Ops:
  7.2 84.3 %all-gather.16.cloned.1.call-start = ((), (), s32[]{:S(2)}) async-start(), calls=%async_computation.10 | async-start | bytes 8519680 | tf_op jit(solution)/shard_map/all_gather | solution.py:57
  7.9 164.1 %all-gather.18.cloned.1.call-start = ((), (), s32[]{:S(2)}) async-start(), calls=%async_computation.11 | async-start | bytes 8519680 | tf_op jit(solution)/shard_map/all_gather | solution.py:58
  8.6 243.8 %all-gather.20.cloned.1.call-start = ((), (), s32[]{:S(2)}) async-start(), calls=%async_computation.12 | async-start | bytes 8519680 | tf_op jit(solution)/shard_map/all_gather | solution.py:59
  9.4 502.2 %all-gather.10.cloned.1.call-start = ((), (), s32[]{:S(2)}) async-start(), calls=%async_computation.3 | async-start | bytes 8519680 | tf_op jit(solution)/shard_map/all_gather | solution.py:92
  270.5 2.3 collective-permute-start
  289.7 3.2 collective-permute-start
  309.8 3.2 collective-permute-start
  329.9 3.2 collective-permute-start
  350.0 3.2 collective-permute-start
  370.2 3.2 collective-permute-start
  390.3 3.2 collective-permute-start
  410.4 3.2 collective-permute-start
  415.9 17.9 collective-permute-start
  433.8 158.1 %all-gather.12.cloned.1.call-start = ((), (), s32[]{:S(2)}) async-start(), calls=%async_computation.4 | async-start | bytes 8519680 | tf_op jit(solution)/shard_map/all_gather | solution.py:91
  434.4 237.9 %all-gather.14.cloned.1.call-start = ((), (), s32[]{:S(2)}) async-start(), calls=%async_computation.5 | async-start | bytes 8519680 | tf_op jit(solution)/shard_map/all_gather | solution.py:90
  435.0 894.7 %all-reduce.2.cloned.1.call-start = ((), (), s32[]{:S(2)}) async-start(), calls=%async_computation.6 | async-start | bytes 2097152 | tf_op jit(solution)/shard_map/psum | solution.py:133
  698.3 64.0 %collective-permute-start.1 = (bf16[64,1024]{1,0:T(8,128)(2,1)S(1)}, bf16[64,1024]{1,0:T(8,128)(2,1)S(1)}, u32[]{:S(2)}, u32[]{:S(2)}) collective-permute-start(bf16[64,1024]{1,0:T(8,128)(2,1)S(1)} %get-tuple-element.544), channel_id=1, source_target_pairs={{1,0},{3,2},{5,4},{7,6},{9,8},{11,10},{13,12},{15,14},{17,16},{19,... | collective-permute-start | bytes 393224 | tf_op jit(solution)/shard_map/while/body/eval_jaxpr/ppermute | solution.py:120
  765.9 14.4 slice-start.6
  783.0 19.7 slice-start
  788.5 14.1 slice-start.3
  806.7 20.1 copy-start
  806.7 20.1 copy-start.2
  826.8 3.2 collective-permute-start.1
  833.7 14.4 slice-start.6
  850.7 19.7 slice-start
  874.4 20.1 copy-start
  874.4 20.1 copy-start.2
  894.6 3.2 collective-permute-start.1
  901.4 14.4 slice-start.6
  918.5 19.7 slice-start
  942.2 20.1 copy-start
  942.2 20.1 copy-start.2
  962.3 3.2 collective-permute-start.1
  969.2 14.4 slice-start.6
  986.2 19.6 slice-start
  991.8 14.1 slice-start.3
  1009.9 20.1 copy-start
  1009.9 20.1 copy-start.2
  1030.1 3.2 collective-permute-start.1
  1036.9 14.4 slice-start.6
  1054.0 19.7 slice-start
  1077.7 20.1 copy-start
  1077.7 20.1 copy-start.2
  1097.8 3.2 collective-permute-start.1
  1104.7 14.4 slice-start.6
  1121.7 19.6 slice-start
  1127.3 14.1 slice-start.3
  1145.4 20.1 copy-start
  1145.4 20.1 copy-start.2
  1165.6 3.2 collective-permute-start.1
  1172.4 14.4 slice-start.6
  1189.5 19.6 slice-start
  1195.0 14.1 slice-start.3
  1213.2 20.1 copy-start
  1213.2 20.1 copy-start.2
  1233.3 3.2 collective-permute-start.1
  1240.2 14.4 slice-start.6
  1257.2 19.7 slice-start
  1280.9 20.1 copy-start
  1280.9 20.1 copy-start.2
  1301.1 3.2 collective-permute-start.1
  1305.4 418.2 %reduce-scatter.8.cloned.1.call-start = ((), (), s32[]{:S(2)}) async-start(), calls=%async_computation.9 | async-start | bytes 17039360 | tf_op jit(solution)/shard_map/reduce_scatter | solution.py:131
  1306.1 807.7 %reduce-scatter.4.cloned.1.call-start = ((), (), s32[]{:S(2)}) async-start(), calls=%async_computation.7 | async-start | bytes 17039360 | tf_op jit(solution)/shard_map/reduce_scatter | solution.py:129
  1306.8 1195.0 %reduce-scatter.6.cloned.1.call-start = ((), (), s32[]{:S(2)}) async-start(), calls=%async_computation.8 | async-start | bytes 17039360 | tf_op jit(solution)/shard_map/reduce_scatter | solution.py:130
  (52 other events, 462.3 us)
Sparse Core Ops, SparseCore 0:
  10.8 80.5 all-gather.15
  94.3 77.6 all-gather.17
  174.8 77.6 all-gather.19
  433.9 77.6 all-gather.9
  514.3 77.6 all-gather.11
  594.7 77.6 all-gather.13
  1305.5 24.1 all-reduce.1
  1332.7 390.8 reduce-scatter.7
  1726.5 387.2 reduce-scatter.3
  2116.6 385.1 reduce-scatter.5
where the time goes:
time: 2510 us
  waiting for transfers between devices  1770 us (71%)
  matrix products  583 us (23%)
  starting transfers between devices  46 us (2%)
  local copies, waits for them, and re-layouts  44 us (2%)
  other arithmetic  43.2 us (2%)
    reduce_scatter x1, waiting for transfers between devices, per_device(): lax.psum_scatter(jnp.stack(grad_sums[2]), 'data', scatter_dimension=1, ti...  394 us
    reduce_scatter x1, waiting for transfers between devices, per_device(): lax.psum_scatter(jnp.stack(grad_sums[0]), 'data', scatter_dimension=1, ti...  390 us
    reduce_scatter x1, waiting for transfers between devices, per_device(): lax.psum_scatter(jnp.stack(grad_sums[1]), 'data', scatter_dimension=1, ti...  388 us
    dot_general x8, matrix products, layer_bwd(): jnp.einsum('td,tf->df', normed, d_gate, preferred_element_type=jnp.float32)  161 us
    dot_general x8, matrix products, layer_bwd(): jnp.einsum('tf,td->fd', hidden, d_next, preferred_element_type=jnp.float32)  113 us
    all_gather x1, waiting for transfers between devices, per_device(): gate_full = lax.all_gather(w_gate[0], 'data', axis=1, tiled=True)  82 us
    all_gather x1, waiting for transfers between devices, per_device(): out_full = lax.all_gather(w_out[0], 'data', axis=1, tiled=True)  80.5 us
    all_gather x1, waiting for transfers between devices, per_device(): in_full = lax.all_gather(w_in[0], 'data', axis=1, tiled=True)  80.5 us
  transfers between devices with their start and end apart: 28, of which 28 were waited for; matrix products, arithmetic and copies ran while one was open for 0% of the time, Pallas kernels for 0%

commit v1 on v0

v1 whole, which is shorter than its diff:
```python
import functools

import jax
import jax.numpy as jnp
from jax import lax
from jax.experimental import pallas as pl
from jax.experimental.pallas import tpu as pltpu
from jax.sharding import PartitionSpec as P

MESH = pl.DeviceIdType.MESH
BF16 = jnp.bfloat16
F32 = jnp.float32
RING = 4
HALF = 128
STEP = 16
WIDE = 1024


class Place:
    def __init__(self, ssem, rsem, lsem):
        d = lax.axis_index('data')
        self.c = c = lax.axis_index('stage')
        self.z = z = d // 16
        self.y = y = (d // 4) % 4
        self.x = x = d % 4
        self.ssem, self.rsem, self.lsem = ssem, rsem, lsem
        self.n_slots = self.n_local = 0
        self.a1, self.a2 = self.order(y, x, c)
        self.z_ring = (z, self.dev((z + 1) % 4, y, x, c), self.dev((z + 3) % 4, y, x, c))
        k = 1 - c
        self.ring1 = (self.a1, self.dev(z, (y + c) % 4, (x + k) % 4, c), self.dev(z, (y + 3 * c) % 4, (x + 3 * k) % 4, c))
        self.ring2 = (self.a2, self.dev(z, (y + k) % 4, (x + c) % 4, c), self.dev(z, (y + 3 * k) % 4, (x + 3 * c) % 4, c))
        self.partner = self.dev(z, y, x, 1 - c)

    @staticmethod
    def order(y, x, c):
        return (1 - c) * x + c * y, (1 - c) * y + c * x

    @staticmethod
    def dev(z, y, x, c):
        return (z * 16 + y * 4 + x, c)

    def slot(self):
        self.n_slots += 1
        return self.n_slots - 1

    def local_slot(self):
        self.n_local += 1
        return self.n_local - 1

    def remote(self, src, dst, dev, slot):
        return pltpu.make_async_remote_copy(src_ref=src, dst_ref=dst, send_sem=self.ssem.at[slot], recv_sem=self.rsem.at[slot], device_id=dev, device_id_type=MESH)

    def push(self, src, dst, dev):
        copy = self.remote(src, dst, dev, self.slot())
        copy.start()
        return copy

    def barrier(self):
        sem = pltpu.get_barrier_semaphore()
        z, y, x, c = self.z, self.y, self.x, self.c
        peers = [self.partner]
        for dz in range(1, 4):
            peers.append(self.dev((z + dz) % 4, y, x, c))
            peers.append(self.dev((z + dz) % 4, y, x, 1 - c))
        peers += [self.ring1[1], self.ring1[2], self.ring2[1], self.ring2[2]]
        for peer in peers:
            pl.semaphore_signal(sem, inc=1, device_id=peer, device_id_type=MESH)
        pl.semaphore_wait(sem, len(peers))


class Gather:
    def __init__(self, place, ring, at):
        self.pl, self.at = place, at
        self.me, self.plus, self.minus = ring

    def start(self):
        me, at, push = self.me, self.at, self.pl.push
        self.p0 = push(at(me, 0), at(me, 0), self.plus)
        self.m1 = push(at(me, 1), at(me, 1), self.minus)
        self.p1 = push(at(me, 1), at(me, 1), self.plus)
        self.m0 = push(at(me, 0), at(me, 0), self.minus)
        return self

    def relay(self):
        before, after = (self.me + 3) % 4, (self.me + 1) % 4
        self.p0.wait_recv()
        self.rp = self.pl.push(self.at(before, 0), self.at(before, 0), self.plus)
        self.m1.wait_recv()
        self.rm = self.pl.push(self.at(after, 1), self.at(after, 1), self.minus)

    def finish(self):
        for copy in (self.p1, self.m0, self.rp, self.rm):
            copy.wait_recv()
        for copy in (self.p0, self.m1, self.p1, self.m0, self.rp, self.rm):
            copy.wait_send()


class Reduce:
    def __init__(self, place, ring, own, held, add):
        self.pl, self.own, self.held, self.add = place, own, held, add
        self.me, self.plus, self.minus = ring

    def start(self):
        me, own, push = self.me, self.own, self.pl.push
        relay, left, right = self.held
        far, after, before = (me + 2) % 4, (me + 1) % 4, (me + 3) % 4
        self.a = push(own(far, 0), relay.at[0], self.plus)
        self.b = push(own(far, 1), relay.at[1], self.minus)
        self.c = push(own(after, 1), left.at[1], self.plus)
        self.d = push(own(before, 0), right.at[0], self.minus)
        return self

    def relay(self):
        relay, left, right = self.held
        after, before = (self.me + 1) % 4, (self.me + 3) % 4
        self.a.wait_recv()
        self.add(relay, 0, after)
        self.e = self.pl.push(relay.at[0], left.at[0], self.plus)
        self.b.wait_recv()
        self.add(relay, 1, before)
        self.f = self.pl.push(relay.at[1], right.at[1], self.minus)

    def finish(self):
        for copy in (self.c, self.d, self.e, self.f):
            copy.wait_recv()
        for copy in (self.a, self.b, self.c, self.d, self.e, self.f):
            copy.wait_send()


def rows_of(i):
    return pl.ds(pl.multiple_of(i * STEP, STEP), STEP)


def by_rows(body):
    for h in range(2):
        def one(i, carry, h=h):
            body(h, rows_of(i))
            return carry
        lax.fori_loop(0, HALF // STEP, one, 0)


def inverse_rms(rows):
    return lax.rsqrt(jnp.mean(rows * rows, axis=-1, keepdims=True) + 1e-6)


def rms(rows):
    return (rows * inverse_rms(rows)).astype(BF16)


def cotangent(h, e, dn):
    r = inverse_rms(h)
    back = r * dn - h * (r * r * r * jnp.mean(h * dn, axis=-1, keepdims=True))
    return (e + back).astype(BF16)


def row_reduce(place, part, held):
    def add(dst, h, j):
        def one(i, carry):
            rows = rows_of(i)
            dst[h, rows] = dst[h, rows] + part[j, h, rows]
            return carry
        lax.fori_loop(0, HALF // STEP, one, 0)
    return Reduce(place, place.z_ring, lambda j, h: part.at[j, h], held, add)


def row_sum(place, part, held, h, rows):
    return part[place.z, h, rows] + held[1][h, rows] + held[2][h, rows]


class Weights:
    def __init__(self, place, s, shards, held, outs):
        self.pl, self.s, self.shards, self.held, self.outs = place, s, shards, held, outs
        self.slots = [[place.slot() for _ in range(2)] for _ in range(4)]
        self.out_slot = place.slot()
        self.swap_slots = [place.slot() for _ in range(3)]
        self.local = [place.local_slot() for _ in range(3)]
        self.copy_local = [place.local_slot() for _ in range(3)]

    def parts(self, dz):
        place = self.pl
        target = (place.z + dz) % 4
        core = place.z // 2
        a1, a2 = place.order(place.y, place.x, core)
        cols = pl.ds(pl.multiple_of(target * WIDE, WIDE), WIDE)
        for m in range(2):
            yield m, self.shards[m].at[:, cols], self.held.at[a1, a2, place.z % 2, m], place.dev(target, place.y, place.x, core)

    def out_part(self, core):
        a1, a2 = self.pl.order(self.pl.y, self.pl.x, core)
        return self.shards[2].at[2 * core:2 * core + 2], self.held.at[a1, a2, :, 2]

    def send(self):
        place, s = self.pl, self.s
        mine = place.z // 2 == s

        @pl.when(place.c == s)
        def _():
            for dz in range(1, 4):
                for m, src, dst, dev in self.parts(dz):
                    place.remote(src, dst, dev, self.slots[dz][m]).start()

            @pl.when(mine)
            def _():
                for m, src, dst, _ in self.parts(0):
                    pltpu.make_async_copy(src, dst, place.lsem.at[self.local[m]]).start()

            @pl.when(jnp.logical_not(mine))
            def _():
                for m, src, dst, _ in self.parts(0):
                    place.remote(src, dst, place.partner, self.slots[0][m]).start()
            src, dst = self.out_part(s)
            pltpu.make_async_copy(src, dst, place.lsem.at[self.local[2]]).start()
            src, dst = self.out_part(1 - s)
            place.remote(src, dst, place.partner, self.out_slot).start()

    def arrive(self):
        place, s = self.pl, self.s
        is_source = place.c == s
        mine = place.z // 2 == s
        for dz in range(4):
            source = (place.z + 4 - dz) % 4
            here = source // 2 == place.c
            if dz == 0:
                here = jnp.logical_and(here, jnp.logical_not(is_source))

            @pl.when(here)
            def _(dz=dz, source=source):
                for m in range(2):
                    dst = self.held.at[place.a1, place.a2, source % 2, m]
                    place.remote(dst, dst, place.partner, self.slots[dz][m]).wait_recv()

        @pl.when(is_source)
        def _():
            for dz in range(1, 4):
                for m, src, dst, dev in self.parts(dz):
                    place.remote(src, dst, dev, self.slots[dz][m]).wait_send()

            @pl.when(mine)
            def _():
                for m, src, dst, _ in self.parts(0):
                    pltpu.make_async_copy(src, dst, place.lsem.at[self.local[m]]).wait()

            @pl.when(jnp.logical_not(mine))
            def _():
                for m, src, dst, _ in self.parts(0):
                    place.remote(src, dst, place.partner, self.slots[0][m]).wait_send()
            src, dst = self.out_part(s)
            pltpu.make_async_copy(src, dst, place.lsem.at[self.local[2]]).wait()
            src, dst = self.out_part(1 - s)
            place.remote(src, dst, place.partner, self.out_slot).wait_send()

        @pl.when(jnp.logical_not(is_source))
        def _():
            _, dst = self.out_part(1 - s)
            place.remote(dst, dst, place.partner, self.out_slot).wait_recv()

    def first(self):
        place, held = self.pl, self.held
        return Gather(place, place.ring2, lambda j, h: held.at[place.a1, j, h]).start()

    def second(self):
        place, held = self.pl, self.held
        return Gather(place, place.ring1, lambda j, h: held.at[j, 2 * h:2 * h + 2]).start()

    def place_of(self, m, p, core):
        if m < 2:
            return self.outs[m].at[pl.ds(2 * core, 2), p]
        return self.outs[m].at[p, pl.ds(2 * core, 2)]

    def half_of(self, m, core):
        if m < 2:
            return self.outs[m].at[pl.ds(2 * core, 2)]
        return self.outs[m].at[:, pl.ds(2 * core, 2)]

    def spread(self):
        place = self.pl

        def one(p, carry):
            a1, a2 = place.order(p // 4, p % 4, place.c)
            for m in range(3):
                src = self.held.at[a1, a2, :, m]
                dst = self.place_of(m, p, place.c)
                place.remote(src, dst, place.partner, self.swap_slots[m]).start()
                pltpu.make_async_copy(src, dst, place.lsem.at[self.copy_local[m]]).start()
            return carry
        lax.fori_loop(0, 16, one, 0)

    def done(self):
        place = self.pl
        for m in range(3):
            mine, other = self.half_of(m, place.c), self.half_of(m, 1 - place.c)
            place.remote(mine, other, place.partner, self.swap_slots[m]).wait_recv()
            place.remote(mine, other, place.partner, self.swap_slots[m]).wait_send()
            pltpu.make_async_copy(mine, mine, place.lsem.at[self.copy_local[m]]).wait()


class Grads:
    def __init__(self, place, s, parts, mine, held1, sum1, held2, sum2, outs):
        self.pl, self.s, self.parts, self.mine = place, s, parts, mine
        self.held1, self.sum1, self.held2, self.sum2, self.outs = held1, sum1, held2, sum2, outs
        self.swap_slots = [place.slot() for _ in range(3)]
        self.slots = [[place.slot() for _ in range(2)] for _ in range(4)]
        self.out_slot = place.slot()
        self.local = [place.local_slot() for _ in range(3)]

    def part(self, m, p, core):
        if m < 2:
            return self.parts[m].at[pl.ds(2 * core, 2), p]
        return self.parts[m].at[p, pl.ds(2 * core, 2)]

    def swap(self):
        place = self.pl

        def one(p, carry):
            other = 1 - place.c
            a1, a2 = place.order(p // 4, p % 4, other)
            for m in range(3):
                place.remote(self.part(m, p, other), self.mine.at[a1, a2, :, m], place.partner, self.swap_slots[m]).start()
            return carry
        lax.fori_loop(0, 16, one, 0)

    def combine(self):
        place, mine = self.pl, self.mine
        for m in range(3):
            whole = mine.at[:, :, :, m]
            place.remote(whole, whole, place.partner, self.swap_slots[m]).wait_recv()

        def one(p, carry):
            a1, a2 = place.order(p // 4, p % 4, place.c)
            for q in range(2):
                for m in range(3):
                    own = self.parts[m][2 * place.c + q, p] if m < 2 else self.parts[m][p, 2 * place.c + q]
                    mine[a1, a2, q, m] = mine[a1, a2, q, m] + own
            return carry
        lax.fori_loop(0, 16, one, 0)
        for m in range(3):
            whole = mine.at[:, :, :, m]
            place.remote(whole, whole, place.partner, self.swap_slots[m]).wait_send()

    def first(self):
        place, mine = self.pl, self.mine

        def add(dst, h, j):
            def one(i, carry):
                k, q = i // 2, i % 2
                for m in range(3):
                    dst[h, k, q, m] = dst[h, k, q, m] + mine[j, 2 * h + k, q, m]
                return carry
            lax.fori_loop(0, 4, one, 0)
        return Reduce(place, place.ring1, lambda j, h: mine.at[j, 2 * h:2 * h + 2], self.held1, add).start()

    def first_sum(self):
        place, mine = self.pl, self.mine
        for h in range(2):
            def one(i, carry, h=h):
                k, q = i // 2, i % 2
                for m in range(3):
                    total = mine[place.a1, 2 * h + k, q, m] + self.held1[1][h, k, q, m] + self.held1[2][h, k, q, m]
                    self.sum1[2 * h + k, q, m] = total
                return carry
            lax.fori_loop(0, 4, one, 0)

    def second(self):
        place, sum1 = self.pl, self.sum1

        def add(dst, h, j):
            for m in range(3):
                dst[h, m] = dst[h, m] + sum1[j, h, m]
        return Reduce(place, place.ring2, lambda j, h: sum1.at[j, h], self.held2, add).start()

    def second_sum(self):
        place = self.pl
        for h in range(2):
            for m in range(3):
                self.sum2[h, m] = self.sum1[place.a2, h, m] + self.held2[1][h, m] + self.held2[2][h, m]

    def shard(self, m, source):
        return self.outs[m].at[:, pl.ds(pl.multiple_of(source * WIDE, WIDE), WIDE)]

    def hand(self, wait):
        place, s = self.pl, self.s
        for dz in range(4):
            target = (place.z + dz) % 4
            to_self = place.c == s

            def go(dz=dz, target=target):
                for m in range(2):
                    copy = place.remote(self.sum2.at[target % 2, m], self.shard(m, place.z), place.dev(target, place.y, place.x, s), self.slots[dz][m])
                    copy.wait_send() if wait else copy.start()

            here = target // 2 == place.c
            if dz:
                pl.when(here)(go)
                continue

            def stay():
                for m in range(2):
                    copy = pltpu.make_async_copy(self.sum2.at[place.z % 2, m], self.shard(m, place.z), place.lsem.at[self.local[m]])
                    copy.wait() if wait else copy.start()
            pl.when(jnp.logical_and(here, to_self))(stay)
            pl.when(jnp.logical_and(here, jnp.logical_not(to_self)))(go)

        rows = self.outs[2].at[pl.ds(2 * place.c, 2)]

        @pl.when(place.c == s)
        def _():
            copy = pltpu.make_async_copy(self.sum2.at[:, 2], rows, place.lsem.at[self.local[2]])
            copy.wait() if wait else copy.start()

        @pl.when(place.c != s)
        def _():
            copy = place.remote(self.sum2.at[:, 2], rows, place.partner, self.out_slot)
            copy.wait_send() if wait else copy.start()

    def done(self):
        place, s = self.pl, self.s

        @pl.when(place.c == s)
        def _():
            for dz in range(4):
                def land(dz=dz):
                    for m in range(2):
                        dst = self.shard(m, (place.z + 4 - dz) % 4)
                        place.remote(dst, dst, place.partner, self.slots[dz][m]).wait_recv()
                if dz:
                    land()
                else:
                    pl.when(place.z // 2 != s)(land)
            dst = self.outs[2].at[pl.ds(2 * (1 - place.c), 2)]
            place.remote(dst, dst, place.partner, self.out_slot).wait_recv()
        self.hand(True)


def kernel_a(x_ref, g_ref, wg, wi, wo, n_ref, ga_ref, og, oi, oo, held_w, ssem, rsem, lsem):
    place = Place(ssem, rsem, lsem)
    place.barrier()
    weights = Weights(place, 0, (wg, wi, wo), held_w, (og, oi, oo))
    weights.send()
    z, c = place.z, place.c
    g_copy = pltpu.make_async_copy(g_ref.at[c], ga_ref.at[z], lsem.at[place.local_slot()])
    g_copy.start()

    def norm(h, rows):
        n_ref[z, h, rows] = rms(x_ref[c, h, rows].astype(F32))
    by_rows(norm)
    rows_n = Gather(place, place.z_ring, lambda j, h: n_ref.at[j, h]).start()
    weights.arrive()
    w_first = weights.first()
    w_first.relay()
    w_first.finish()
    w_second = weights.second()
    rows_n.relay()
    g_copy.wait()
    rows_g = Gather(place, place.z_ring, lambda j, h: ga_ref.at[j, h]).start()
    w_second.relay()
    rows_n.finish()
    w_second.finish()
    weights.spread()
    rows_g.relay()
    rows_g.finish()
    weights.done()


def kernel_b(part, x_ref, wg, wi, wo, h_ref, n_ref, og, oi, oo, held, left, right, held_w, ssem, rsem, lsem):
    place = Place(ssem, rsem, lsem)
    place.barrier()
    bufs = (held, left, right)
    weights = Weights(place, 1, (wg, wi, wo), held_w, (og, oi, oo))
    weights.send()
    rows_o = row_reduce(place, part, bufs).start()
    weights.arrive()
    w_first = weights.first()
    w_first.relay()
    w_first.finish()
    w_second = weights.second()
    rows_o.relay()
    w_second.relay()
    w_second.finish()
    weights.spread()
    rows_o.finish()
    z, c = place.z, place.c

    def step(h, rows):
        o = row_sum(place, part, bufs, h, rows).astype(BF16).astype(F32)
        out = (x_ref[c, h, rows].astype(F32) + o).astype(BF16)
        h_ref[h, rows] = out
        n_ref[z, h, rows] = rms(out.astype(F32))
    by_rows(step)
    rows_n = Gather(place, place.z_ring, lambda j, h: n_ref.at[j, h]).start()
    rows_n.relay()
    rows_n.finish()
    weights.done()


def kernel_c(part, h_ref, g_ref, dg, di, do, wg, wi, wo, e_ref, eo_ref, og, oi, oo, gg, gi, go, held, left, right, held_w, mine, h1, l1, r1, sum1, h2, l2, r2, sum2, ssem, rsem, lsem):
    place = Place(ssem, rsem, lsem)
    place.barrier()
    bufs = (held, left, right)
    z, c = place.z, place.c
    weights = Weights(place, 0, (wg, wi, wo), held_w, (og, oi, oo))
    grads = Grads(place, 1, (dg, di, do), mine, (h1, l1, r1), sum1, (h2, l2, r2), sum2, (gg, gi, go))
    weights.send()
    rows_d = row_reduce(place, part, bufs).start()
    grads.swap()
    weights.arrive()
    w_first = weights.first()
    w_first.relay()
    w_first.finish()
    w_second = weights.second()
    grads.combine()
    g_first = grads.first()
    rows_d.relay()
    w_second.relay()
    g_first.relay()
    w_second.finish()
    weights.spread()
    rows_d.finish()

    def step(h, rows):
        dn = row_sum(place, part, bufs, h, rows)
        e = cotangent(h_ref[h, rows].astype(F32), g_ref[c, h, rows].astype(F32), dn)
        e_ref[z, h, rows] = e
        eo_ref[h, rows] = e
    by_rows(step)
    rows_e = Gather(place, place.z_ring, lambda j, h: e_ref.at[j, h]).start()
    g_first.finish()
    grads.first_sum()
    g_second = grads.second()
    rows_e.relay()
    g_second.relay()
    g_second.finish()
    grads.second_sum()
    grads.hand(False)
    rows_e.finish()
    weights.done()
    grads.done()


def kernel_d(part, x_ref, e_ref, dg, di, do, dx_ref, gg, gi, go, held, left, right, mine, h1, l1, r1, sum1, h2, l2, r2, sum2, ssem, rsem, lsem):
    place = Place(ssem, rsem, lsem)
    place.barrier()
    bufs = (held, left, right)
    c = place.c
    grads = Grads(place, 0, (dg, di, do), mine, (h1, l1, r1), sum1, (h2, l2, r2), sum2, (gg, gi, go))
    grads.swap()
    rows_d = row_reduce(place, part, bufs).start()
    grads.combine()
    g_first = grads.first()
    rows_d.relay()
    g_first.relay()
    rows_d.finish()

    def step(h, rows):
        dn = row_sum(place, part, bufs, h, rows)
        dx_ref[c, h, rows] = cotangent(x_ref[c, h, rows].astype(F32), e_ref[h, rows].astype(F32), dn)
    by_rows(step)
    swap = place.push(dx_ref.at[c], dx_ref.at[c], place.partner)
    g_first.finish()
    grads.first_sum()
    g_second = grads.second()
    g_second.relay()
    g_second.finish()
    grads.second_sum()
    grads.hand(False)
    swap.wait()
    grads.done()


VM = pl.BlockSpec(memory_space=pltpu.VMEM)
ANY = pl.BlockSpec(memory_space=pl.ANY)


def sds(shape, dtype):
    return jax.ShapeDtypeStruct(shape, dtype)


ALL_ROWS = (4, 2, HALF, WIDE)
OWN_ROWS = (2, HALF, WIDE)
W_SHAPES = [sds((4, 16, 16, WIDE), BF16), sds((4, 16, 16, WIDE), BF16), sds((16, 4, 16, WIDE), BF16)]
G_SHAPES = [sds((16, 4 * WIDE), F32), sds((16, 4 * WIDE), F32), sds((4, 16, WIDE), F32)]
ROW_BUFS = [pltpu.VMEM(OWN_ROWS, F32)] * 3
W_BUFS = [pltpu.VMEM((4, 4, 2, 3, 16, WIDE), BF16)]
G_BUFS = (
    [pltpu.VMEM((4, 4, 2, 3, 16, WIDE), F32)]
    + [pltpu.VMEM((2, 2, 2, 3, 16, WIDE), F32)] * 3
    + [pltpu.VMEM((4, 2, 3, 16, WIDE), F32)]
    + [pltpu.VMEM((2, 3, 16, WIDE), F32)] * 3
    + [pltpu.VMEM((2, 3, 16, WIDE), F32)]
)
SEMS = [pltpu.SemaphoreType.DMA((64,)), pltpu.SemaphoreType.DMA((64,)), pltpu.SemaphoreType.DMA((16,))]


def call(kernel, cid, n_in, outs, out_specs, scratch):
    return pl.pallas_call(
        kernel,
        out_shape=outs,
        in_specs=[VM] * n_in,
        out_specs=out_specs,
        scratch_shapes=scratch + SEMS,
        compiler_params=pltpu.CompilerParams(collective_id=cid, has_side_effects=True, vmem_limit_bytes=60 * 1024 * 1024),
        name=kernel.__name__,
    )


def mm(a, b):
    return jnp.dot(a, b, preferred_element_type=F32)


def mm_t(a, b):
    return lax.dot_general(a, b, (((0,), (0,)), ((), ())), preferred_element_type=F32)


def mm_nt(a, b):
    return lax.dot_general(a, b, (((1,), (1,)), ((), ())), preferred_element_type=F32)


def flat(t):
    return t.reshape(-1, WIDE)


def backward(n, a, b, u, e, gate, inn, out):
    s = jax.nn.sigmoid(a)
    d_out = mm_t(u, e)
    t = mm_nt(e, out)
    da = (t * b * s * (1.0 + a * (1.0 - s))).astype(BF16)
    db = (t * (a * s)).astype(BF16)
    dn = mm_nt(da, gate) + mm_nt(db, inn)
    d_gate = mm_t(n, da)
    d_in = mm_t(n, db)
    grads = (d_gate.reshape(4, 16, 16, WIDE), d_in.reshape(4, 16, 16, WIDE), d_out.reshape(16, 4, 16, WIDE))
    return dn.reshape(ALL_ROWS), grads


def hidden(n, gate, inn):
    a, b = mm(n, gate), mm(n, inn)
    return a, b, (a * jax.nn.sigmoid(a) * b).astype(BF16)


def solution(mesh):
    act_spec = P(None, 'data', None, None)
    weight_spec = P('stage', None, 'data', None)

    def per_device(x, g, w_gate, w_in, w_out):
        xs = x.reshape(2, 2, HALF, WIDE)
        gs = g.reshape(2, 2, HALF, WIDE)
        shards = (w_gate.reshape(16, 4 * WIDE), w_in.reshape(16, 4 * WIDE), w_out.reshape(4, 16, WIDE))

        n0, g_all, *w0 = call(kernel_a, 1, 5, [sds(ALL_ROWS, BF16)] * 2 + W_SHAPES, [VM] * 2 + [ANY] * 3, W_BUFS)(xs, gs, *shards)
        n0, g_all = flat(n0), flat(g_all)
        a0, b0, u0 = hidden(n0, flat(w0[0]), flat(w0[1]))
        o0 = mm(u0, flat(w0[2])).reshape(ALL_ROWS)

        h1, n1, *w1 = call(kernel_b, 2, 5, [sds(OWN_ROWS, BF16), sds(ALL_ROWS, BF16)] + W_SHAPES, [VM] * 2 + [ANY] * 3, ROW_BUFS + W_BUFS)(o0, xs, *shards)
        n1 = flat(n1)
        w1 = [flat(w) for w in w1]
        a1, b1, u1 = hidden(n1, w1[0], w1[1])
        dn1, grads1 = backward(n1, a1, b1, u1, g_all, *w1)

        outs = [sds(ALL_ROWS, BF16), sds(OWN_ROWS, BF16)] + W_SHAPES + G_SHAPES
        e_all, e_own, *rest = call(kernel_c, 3, 9, outs, [VM] * 2 + [ANY] * 3 + [VM] * 3, ROW_BUFS + W_BUFS + G_BUFS)(dn1, h1, gs, *grads1, *shards)
        w0 = [flat(w) for w in rest[:3]]
        dn0, grads0 = backward(n0, a0, b0, u0, flat(e_all), *w0)

        outs = [sds((2, 2, HALF, WIDE), BF16)] + G_SHAPES
        dx, *own0 = call(kernel_d, 4, 6, outs, [VM] * 4, ROW_BUFS + G_BUFS)(dn0, xs, e_own, *grads0)
        first = lax.axis_index('stage') == 0
        own = [jnp.where(first, s0, s1) for s0, s1 in zip(own0, rest[3:])]
        return (dx.reshape(x.shape), own[0].reshape(w_gate.shape), own[1].reshape(w_in.shape), own[2].reshape(w_out.shape))

    return jax.shard_map(per_device, mesh=mesh, in_specs=(act_spec, act_spec, weight_spec, weight_spec, weight_spec), out_specs=(act_spec, weight_spec, weight_spec, weight_spec), check_vma=False)
```

time: 2510 us -> 411 us (0.16)
  waiting for transfers between devices: 1770 us -> 0 us
  matrix products: 583 us -> 83.6 us
  Pallas kernels: 0 us -> 265 us
  starting transfers between devices: 46 us -> 0 us
  other arithmetic: 43.2 us -> 13.3 us
    reduce_scatter x3 -> x0, waiting for transfers between devices: 1170 us -> none  [the longest x1 394 us: per_device(): lax.psum_scatter(jnp.stack(grad_sums[2]), 'data', scatter_dimension=1, ti...]
    dot_general x80 -> x17, matrix products: 583 us -> 83.6 us  [the longest x6 28.7 us: mm_t(): lax.dot_general(a, b, (((0,), (0,)), ((), ())), preferred_element_type=F32)]
    all_gather x6 -> x0, waiting for transfers between devices: 480 us -> none  [the longest x1 82 us: per_device(): gate_full = lax.all_gather(w_gate[0], 'data', axis=1, tiled=True)]
    pallas_call x0 -> x4, Pallas kernels: none -> 265 us  [the longest x1 79.9 us: per_device(): call(kernel_c, 3, 9, outs, [VM] * 2 + [ANY] * 3 + [VM] * 3, ROW_BUFS + W_...]
    ppermute x18 -> x0, waiting for transfers between devices: 86.8 us -> none  [the longest x9 78.2 us: bwd_tick(): sent_out = lax.ppermute(d_in, 'stage', bwd_pairs)]
    ppermute x18 -> x0, starting transfers between devices: 45.6 us -> none  [the longest x9 34 us: fwd_tick(): sent_out = lax.ppermute(block_out, 'stage', fwd_pairs)]
    dot_general x0 -> x7, local copies, waits for them, and re-layouts: none -> 30.9 us  [the longest x5 24.2 us: mm(): return jnp.dot(a, b, preferred_element_type=F32)]
  transfers between devices with their start and end apart: 28 -> 0, of which waited for: 28 -> 0; matrix products, arithmetic and copies ran while one was open for 0% -> 0% of each run, Pallas kernels for 0% -> 0%
where the time goes in v1:
time: 411 us; the launch traced here: 403 us
  Pallas kernels  265 us (64%)
  matrix products  83.6 us (20%)
  local copies, waits for them, and re-layouts  40.2 us (10%)
  other arithmetic  13.3 us (3%)
    pallas_call x1, Pallas kernels, per_device(): call(kernel_c, 3, 9, outs, [VM] * 2 + [ANY] * 3 + [VM] * 3, ROW_BUFS + W_...  79.9 us
    pallas_call x1, Pallas kernels, per_device(): call(kernel_d, 4, 6, outs, [VM] * 4, ROW_BUFS + G_BUFS)  71.3 us
    pallas_call x1, Pallas kernels, per_device(): call(kernel_b, 2, 5, [sds(OWN_ROWS, BF16), sds(ALL_ROWS, BF16)] + W_SHAPE...  65.1 us
    pallas_call x1, Pallas kernels, per_device(): call(kernel_a, 1, 5, [sds(ALL_ROWS, BF16)] * 2 + W_SHAPES, [VM] * 2 + [AN...  48.8 us
    dot_general x6, matrix products, mm_t(): lax.dot_general(a, b, (((0,), (0,)), ((), ())), preferred_element_type=F32)  28.7 us
    dot_general x5, matrix products, mm(): return jnp.dot(a, b, preferred_element_type=F32)  27.9 us
    dot_general x6, matrix products, mm_nt(): lax.dot_general(a, b, (((1,), (1,)), ((), ())), preferred_element_type=F32)  26.9 us
    dot_general x5, local copies, waits for them, and re-layouts, mm(): return jnp.dot(a, b, preferred_element_type=F32)  24.2 us

profile of v1, /device:TPU:0, one launch (start us, length us, event | category | flops | bytes accessed | tf_op | source)
XLA Modules:
  0.0 403.3 jit_solution(445408004176398727)
XLA Ops:
  0.6 48.8 %kernel_a.1 = (bf16[4,2,128,1024]{3,2,1,0:T(8,128)(2,1)}, bf16[4,2,128,1024]{3,2,1,0:T(8,128)(2,1)}, bf16[4,16,16,1024]{3,2,1,0:T(8,128)(2,1)}, bf16[4,16,16,102...) custom-call(bf16[2,2,128,1024]{3,2,1,0:T(8,128)(2,1)} %bitcast.123, bf16[2,2,128,1024]{3,2,1,0:T(8,128)(2,1)} %bitcast.126, ...), custom_call_target="tpu_custom_call" | custom-call | tf_op jit(solution)/shard_map/kernel_a/pallas_call | solution.py:649
  49.4 0.0 copy-start.5
  49.4 6.7 %fusion.17 = f32[1024,1024]{1,0:T(8,128)} fusion(bf16[1024,1024]{1,0:T(8,128)(2,1)} %bitcast.135, bf16[1024,1024]{1,0:T(8,128)(2,1)} %bitcast.168), kind=kOutput, calls=%fused_computation.35 | convolution fusion | flops 2147483648 | bytes 8388608 | tf_op jit(solution)/shard_map/dot_general | solution.py:607
  56.1 0.0 copy-done.5
  56.1 2.7 copy.45
  58.8 5.3 %copy.30 = f32[1024,1024]{0,1:T(8,128)} copy(f32[1024,1024]{1,0:T(8,128)} %fusion.17) | data formatting | bytes 8388608 | tf_op jit(solution)/shard_map/dot_general | solution.py:607
  64.1 8.0 %fusion = (bf16[1024,1024]{0,1:T(8,128)(2,1)}, f32[1024,1024]{1,0:T(8,128)}) fusion(f32[1024,1024]{1,0:T(8,128)} %fusion.17, bf16[1024,1024]{1,0:T(8,128)(2,1)S(1)} %bitcast.137, bf16[1024,1024]{1,0:T(8,128)(2,1)} %bitcast.167), kind=kOutput, calls=%fused_computation.1 | convolution fusion | flops 2153775104 | bytes 14680064 | tf_op jit(solution)/shard_map/dot_general | solution.py:607
  72.2 4.0 copy.48
  76.1 5.5 %copy.31 = f32[1024,1024]{0,1:T(8,128)} copy(f32[1024,1024]{1,0:T(8,128)} %get-tuple-element.53) | data formatting | bytes 8388608 | tf_op jit(solution)/shard_map/dot_general | solution.py:607
  81.6 4.8 %multiply_convert_fusion.4 = bf16[1024,1024]{0,1:T(8,128)(2,1)S(1)} fusion(f32[1024,1024]{0,1:T(8,128)} %copy.31, f32[1024,1024]{0,1:T(8,128)} %copy.30), kind=kLoop, calls=%fused_computation.19 | loop fusion | flops 6291456 | bytes 10485760 | tf_op jit(solution)/shard_map/convert_element_type | solution.py:637
  86.4 2.7 copy.58
  89.1 6.5 %fusion.18.part = f32[4,2,128,1024]{3,2,1,0:T(8,128)} fusion(bf16[4,2,128,1024]{3,2,1,0:T(8,128)(2,1)} %bitcast.141, bf16[1024,1024,1,1]{1,0,3,2:T(8,128)(2,1)} %bitcast.162), kind=kOutput, calls=%fused_computation.36 | convolution fusion | flops 2147483648 | bytes 8388608 | tf_op jit(solution)/shard_map/dot_general | solution.py:607
  95.6 65.1 %kernel_b.1 = (bf16[2,128,1024]{2,1,0:T(8,128)(2,1)}, bf16[4,2,128,1024]{3,2,1,0:T(8,128)(2,1)}, bf16[4,16,16,1024]{3,2,1,0:T(8,128)(2,1)}, bf16[4,16,16,1024]{3,2,1,0:T(8,128)(2,1)}, bf16[16,4,16,1024]{3,2,1,0:T(8,128)(2,1)}) custom-call(f32[4,2,128,1024]{3,2,1,0:T(8,128)} %fusion.18.part, bf16[2,2,128,1024]{3,2,1,0:T(8,128)(2,1)} %bitcast.124, ...), custom_call_target="tpu_custom_call" | custom-call | tf_op jit(solution)/shard_map/kernel_b/pallas_call | solution.py:654
  160.7 0.0 copy-start.6
  160.7 4.1 %copy.35 = bf16[1024,1024]{1,0:T(8,128)(2,1)} copy(bf16[1024,1024]{0,1:T(8,128)(2,1)} %bitcast.138) | data formatting | bytes 4194304 | tf_op jit(solution)/shard_map/dot_general | solution.py:611
  164.8 0.0 copy-done.6
  164.8 4.2 %fusion.19 = f32[1024,1024]{0,1:T(8,128)S(1)} fusion(bf16[1024,1024]{1,0:T(8,128)(2,1)S(1)} %bitcast.139, bf16[1024,1024]{1,0:T(8,128)(2,1)} %bitcast.158), kind=kOutput, calls=%fused_computation.37 | convolution fusion | flops 2147483648 | bytes 8388608 | tf_op jit(solution)/shard_map/dot_general | solution.py:607
  169.1 0.0 copy-done.14
  169.1 0.0 copy-start.1
  169.1 0.0 copy-start.11
  169.1 0.0 copy-start.18
  169.1 2.5 fusion.20
  171.6 0.0 copy-done.1
  171.6 0.6 copy-done.11
  172.2 0.6 copy-done.18
  172.8 5.1 %multiply_convert_fusion.2 = (bf16[1024,1024]{0,1:T(8,128)(2,1)}, bf16[1024,1024]{0,1:T(8,128)(2,1)}) fusion(f32[1024,1024]{0,1:T(8,128)S(1)} %fusion.20, f32[1024,1024]{0,1:T(8,128)S(1)} %fusion.19, bf16[1024,1024]{1,0:T(8,128)(2,1)S(1)} %bitcast.155, bf16[1024,1024]{1,0:T(8,128)(2,1)S(1)} %bitcast.166), kind=kOutput, calls=%fused_computation.16 | convolution fusion | flops 2161115136 | bytes 16777216 | tf_op jit(solution)/shard_map/dot_general | solution.py:615
  178.0 0.0 copy-done
  178.0 5.3 %copy.39 = f32[1024,1024]{1,0:T(8,128)} copy(f32[1024,1024]{0,1:T(8,128)} %copy-done.1) | data formatting | bytes 8388608 | tf_op jit(solution)/shard_map/dot_general | solution.py:607
  183.3 5.4 %copy.38 = f32[1024,1024]{1,0:T(8,128)} copy(f32[1024,1024]{0,1:T(8,128)} %copy-done) | data formatting | bytes 8388608 | tf_op jit(solution)/shard_map/dot_general | solution.py:607
  188.7 4.8 %fusion.4 = bf16[1024,1024]{0,1:T(8,128)(2,1)S(1)} fusion(f32[1024,1024]{1,0:T(8,128)} %copy.39, f32[1024,1024]{1,0:T(8,128)} %copy.38), kind=kLoop, calls=%fused_computation.8 | loop fusion | flops 6291456 | bytes 10485760 | tf_op jit(solution)/shard_map/convert_element_type | solution.py:637
  193.5 3.0 copy.40
  196.6 0.0 copy-start.15
  196.6 0.0 copy-start.20
  196.6 6.7 %fusion.22.do = f32[16,4,16,1024]{3,2,1,0:T(8,128)} fusion(bf16[16,4,16,1024]{3,2,1,0:T(8,128)(2,1)} %bitcast.142, bf16[1024,1024,1,1]{1,0,3,2:T(8,128)(2,1)} %bitcast.154), kind=kOutput, calls=%fused_computation.40 | convolution fusion | flops 2147483648 | bytes 8388608 | tf_op jit(solution)/shard_map/dot_general | solution.py:611
  203.3 0.0 copy-done.15
  203.3 0.0 copy-done.20
  203.3 0.0 copy-start.19
  203.3 2.4 fusion.21
  205.7 0.0 copy-done.13
  205.7 0.0 copy-done.19
  205.7 0.0 copy-start.4
  205.7 4.3 %convolution_add_fusion.1 = f32[1024,1024]{1,0:T(8,128)} fusion(f32[1024,1024]{1,0:T(8,128)S(1)} %fusion.21, bf16[1024,1024]{0,1:T(8,128)(2,1)S(1)} %copy-done.19, bf16[1024,1024]{1,0:T(8,128)(2,1)S(1)} %bitcast.159), kind=kOutput, calls=%fused_computation.31 | convolution fusion | flops 2148532224 | bytes 12582912 | tf_op jit(solution)/shard_map/dot_general | solution.py:615
  210.1 0.0 copy-done.4
  210.1 4.4 %fusion.13.di = f32[4,16,16,1024]{3,2,1,0:T(8,128)} fusion(bf16[4,16,16,1024]{3,2,1,0:T(8,128)(2,1)S(1)} %bitcast.133, bf16[1024,1024]{0,1:T(8,128)(2,1)S(1)} %copy-done.19), kind=kOutput, calls=%fused_computation.26 | convolution fusion | flops 2147483648 | bytes 8388608 | tf_op jit(solution)/shard_map/dot_general | solution.py:611
  214.5 4.3 %fusion.15.dg = f32[4,16,16,1024]{3,2,1,0:T(8,128)} fusion(bf16[4,16,16,1024]{3,2,1,0:T(8,128)(2,1)S(1)} %bitcast.134, bf16[1024,1024]{0,1:T(8,128)(2,1)S(1)} %copy-done.20), kind=kOutput, calls=%fused_computation.28 | convolution fusion | flops 2147483648 | bytes 8388608 | tf_op jit(solution)/shard_map/dot_general | solution.py:611
  218.8 79.9 %kernel_c.1 = (bf16[4,2,128,1024]{3,2,1,0:T(8,128)(2,1)}, bf16[2,128,1024]{2,1,0:T(8,128)(2,1)}, bf16[4,16,16,1024]{3,2,1,0:T(8,128)(2,1)}, bf16[4,16,16,1024]{3...) custom-call(f32[4,2,128,1024]{3,2,1,0:T(8,128)} %bitcast.128, ...), custom_call_target="tpu_custom_call" | custom-call | tf_op jit(solution)/shard_map/kernel_c/pallas_call | solution.py:661
  298.7 0.0 copy-start.17
  298.7 8.3 %multiply_convert_fusion = (bf16[1024,1024]{0,1:T(8,128)(2,1)S(1)}, bf16[1024,1024]{0,1:T(8,128)(2,1)S(1)}) fusion(f32[1024,1024]{0,1:T(8,128)} %copy.30, f32[1024,1024]{0,1:T(8,128)} %copy.31, bf16[1024,1024]{1,0:T(8,128)(2,1)} %bitcast.156, bf16[1024,1024]{1,0:T(8,128)(2,1)} %bitcast.165), kind=kOutput, calls=%fused_computation.14 | convolution fusion | flops 2161115136 | bytes 16777216 | tf_op jit(solution)/shard_map/dot_general | solution.py:615
  307.0 0.0 copy-done.17
  307.0 0.0 copy-start.16
  307.0 2.4 fusion.23
  309.4 0.0 copy-done.16
  309.4 0.0 copy-start.2
  309.4 4.4 %convolution_add_fusion = f32[1024,1024]{1,0:T(8,128)} fusion(f32[1024,1024]{1,0:T(8,128)S(1)} %fusion.23, bf16[1024,1024]{0,1:T(8,128)(2,1)S(1)} %get-tuple-element.48, bf16[1024,1024]{1,0:T(8,128)(2,1)S(1)} %bitcast.163), kind=kOutput, calls=%fused_computation.30 | convolution fusion | flops 2148532224 | bytes 12582912 | tf_op jit(solution)/shard_map/dot_general | solution.py:615
  313.8 0.0 copy-done.2
  313.8 4.4 %fusion.9.di = f32[4,16,16,1024]{3,2,1,0:T(8,128)} fusion(bf16[4,16,16,1024]{3,2,1,0:T(8,128)(2,1)S(1)} %bitcast.130, bf16[1024,1024]{0,1:T(8,128)(2,1)S(1)} %get-tuple-element.48), kind=kOutput, calls=%fused_computation.22 | convolution fusion | flops 2147483648 | bytes 8388608 | tf_op jit(solution)/shard_map/dot_general | solution.py:611
  318.2 4.6 %fusion.11.dg = f32[4,16,16,1024]{3,2,1,0:T(8,128)} fusion(bf16[4,16,16,1024]{3,2,1,0:T(8,128)(2,1)S(1)} %bitcast.131, bf16[1024,1024]{0,1:T(8,128)(2,1)S(1)} %get-tuple-element.49), kind=kOutput, calls=%fused_computation.24 | convolution fusion | flops 2147483648 | bytes 8388608 | tf_op jit(solution)/shard_map/dot_general | solution.py:611
  322.8 0.0 copy-done.3
  322.8 0.0 copy-done.12
  322.8 4.3 %fusion.24.do = f32[16,4,16,1024]{3,2,1,0:T(8,128)} fusion(bf16[16,4,16,1024]{3,2,1,0:T(8,128)(2,1)S(1)} %bitcast.132, bf16[1024,1024,1,1]{1,0,3,2:T(8,128)(2,1)S(1)} %bitcast.157), kind=kOutput, calls=%fused_computation.42 | convolution fusion | flops 2147483648 | bytes 8388608 | tf_op jit(solution)/shard_map/dot_general | solution.py:611
  327.1 71.3 %kernel_d.1 = (bf16[2,2,128,1024]{3,2,1,0:T(8,128)(2,1)}, f32[16,4096]{1,0:T(8,128)}, f32[16,4096]{1,0:T(8,128)}, f32[4,16,1024]{2,1,0:T(8,128)}) custom-call(f32[4,2,128,1024]{3,2,1,0:T(8,128)} %bitcast.129, bf16[2,2,128,1024]{3,2,1,0:T(8,128)(2,1)} %bitcast.125, bf16[2,128,1024]{2,1,0:T(8,128)(2,1)} %get-tuple-element.40.e_ref, ...), custom_call_target="tpu_custom_call" | custom-call | tf_op jit(solution)/shard_map/kernel_d/pallas_call | solution.py:666
  398.4 1.8 broadcast_select_fusion
  400.2 1.9 select_bitcast_fusion
  402.1 1.0 copy.64
  (13 shorter events, 0.0 us)
Async XLA Ops:
  49.4 6.7 %copy-start.5 = (bf16[4,2,128,1024]{3,2,1,0:T(8,128)(2,1)S(1)}, bf16[4,2,128,1024]{3,2,1,0:T(8,128)(2,1)}, u32[]{:S(2)}) copy-start(bf16[4,2,128,1024]{3,2,1,0:T(8,128)(2,1)} %get-tuple-element.27) | copy-start | bytes 6291460
  160.7 4.1 %copy-start.6 = (bf16[4,2,128,1024]{3,2,1,0:T(8,128)(2,1)S(1)}, bf16[4,2,128,1024]{3,2,1,0:T(8,128)(2,1)}, u32[]{:S(2)}) copy-start(bf16[4,2,128,1024]{3,2,1,0:T(8,128)(2,1)} %get-tuple-element.32) | copy-start | bytes 6291460
  164.8 4.2 %copy-start.14 = (bf16[4,16,16,1024]{3,2,1,0:T(8,128)(2,1)S(1)}, bf16[4,16,16,1024]{3,2,1,0:T(8,128)(2,1)}, u32[]{:S(2)}) copy-start(bf16[4,16,16,1024]{3,2,1,0:T(8,128)(2,1)} %get-tuple-element.34) | copy-start | bytes 6291460
  169.1 2.5 copy-start.1
  169.1 3.1 copy-start.11
  169.1 3.7 copy-start.18
  172.8 5.1 %copy-start = (f32[1024,1024]{0,1:T(8,128)}, f32[1024,1024]{0,1:T(8,128)S(1)}, u32[]{:S(2)}) copy-start(f32[1024,1024]{0,1:T(8,128)S(1)} %fusion.20) | copy-start | bytes 12582916
  196.6 6.7 %copy-start.15 = (bf16[4,16,16,1024]{3,2,1,0:T(8,128)(2,1)S(1)}, bf16[4,16,16,1024]{3,2,1,0:T(8,128)(2,1)}, u32[]{:S(2)}) copy-start(bf16[4,16,16,1024]{3,2,1,0:T(8,128)(2,1)} %get-tuple-element.34) | copy-start | bytes 6291460
  196.6 6.7 %copy-start.20 = (bf16[1024,1024]{0,1:T(8,128)(2,1)S(1)}, bf16[1024,1024]{0,1:T(8,128)(2,1)}, u32[]{:S(2)}) copy-start(bf16[1024,1024]{0,1:T(8,128)(2,1)} %get-tuple-element.51) | copy-start | bytes 6291460
  203.3 2.4 copy-start.13
  203.3 2.4 copy-start.19
  205.7 4.3 %copy-start.4 = (bf16[1024,1024]{1,0:T(8,128)(2,1)S(1)}, bf16[1024,1024]{1,0:T(8,128)(2,1)}, u32[]{:S(2)}) copy-start(bf16[1024,1024]{1,0:T(8,128)(2,1)} %copy.35) | copy-start | bytes 6291460
  298.7 8.3 %copy-start.17 = (bf16[4,16,16,1024]{3,2,1,0:T(8,128)(2,1)S(1)}, bf16[4,16,16,1024]{3,2,1,0:T(8,128)(2,1)}, u32[]{:S(2)}) copy-start(bf16[4,16,16,1024]{3,2,1,0:T(8,128)(2,1)} %get-tuple-element.38) | copy-start | bytes 6291460
  307.0 2.4 copy-start.16
  309.4 4.4 %copy-start.2 = (bf16[1024,1024]{1,0:T(8,128)(2,1)S(1)}, bf16[1024,1024]{1,0:T(8,128)(2,1)}, u32[]{:S(2)}) copy-start(bf16[1024,1024]{1,0:T(8,128)(2,1)} %copy.45) | copy-start | bytes 6291460
  318.2 4.6 %copy-start.3 = (bf16[1024,1024]{1,0:T(8,128)(2,1)S(1)}, bf16[1024,1024]{1,0:T(8,128)(2,1)}, u32[]{:S(2)}) copy-start(bf16[1024,1024]{1,0:T(8,128)(2,1)} %copy.48) | copy-start | bytes 6291460
  318.2 4.6 %copy-start.12 = (bf16[4,2,128,1024]{3,2,1,0:T(8,128)(2,1)S(1)}, bf16[4,2,128,1024]{3,2,1,0:T(8,128)(2,1)}, u32[]{:S(2)}) copy-start(bf16[4,2,128,1024]{3,2,1,0:T(8,128)(2,1)} %get-tuple-element.36) | copy-start | bytes 6291460
  327.1 71.3 %copy-start.10 = (f32[4,16,1024]{2,1,0:T(8,128)S(1)}, f32[4,16,1024]{2,1,0:T(8,128)}, u32[]{:S(2)}) copy-start(f32[4,16,1024]{2,1,0:T(8,128)} %get-tuple-element.47) | copy-start | bytes 786436
  327.1 73.1 %copy-start.8 = (f32[16,4096]{1,0:T(8,128)S(1)}, f32[16,4096]{1,0:T(8,128)}, u32[]{:S(2)}) copy-start(f32[16,4096]{1,0:T(8,128)} %get-tuple-element.43) | copy-start | bytes 786436
  327.1 73.1 %copy-start.9 = (f32[16,4096]{1,0:T(8,128)S(1)}, f32[16,4096]{1,0:T(8,128)}, u32[]{:S(2)}) copy-start(f32[16,4096]{1,0:T(8,128)} %get-tuple-element.45) | copy-start | bytes 786436
  398.4 3.7 copy-start.7

commit v2 on v0

v2 whole, which is shorter than its diff:
```python
import functools

import jax
import jax.numpy as jnp
from jax import lax
from jax.experimental import pallas as pl
from jax.experimental.pallas import tpu as pltpu
from jax.sharding import PartitionSpec as P

MESH = pl.DeviceIdType.MESH
BF16 = jnp.bfloat16
F32 = jnp.float32
RING = 4
CHUNKS = 4
HALF = 128 // CHUNKS
ROWS = 8 * HALF
STEP = 16
COLS = 512
WIDE = 1024
N_REMOTE = 160
N_LOCAL = 32


class Place:
    def __init__(self, ssem, rsem, lsem):
        d = lax.axis_index('data')
        self.c = c = lax.axis_index('stage')
        self.z = z = d // 16
        self.y = y = (d // 4) % 4
        self.x = x = d % 4
        self.ssem, self.rsem, self.lsem = ssem, rsem, lsem
        self.n_slots = self.n_local = 0
        self.a1, self.a2 = self.order(y, x, c)
        self.z_ring = (z, self.dev((z + 1) % 4, y, x, c), self.dev((z + 3) % 4, y, x, c))
        k = 1 - c
        self.ring1 = (self.a1, self.dev(z, (y + c) % 4, (x + k) % 4, c), self.dev(z, (y + 3 * c) % 4, (x + 3 * k) % 4, c))
        self.ring2 = (self.a2, self.dev(z, (y + k) % 4, (x + c) % 4, c), self.dev(z, (y + 3 * k) % 4, (x + 3 * c) % 4, c))
        self.partner = self.dev(z, y, x, 1 - c)

    @staticmethod
    def order(y, x, c):
        return (1 - c) * x + c * y, (1 - c) * y + c * x

    @staticmethod
    def dev(z, y, x, c):
        return (z * 16 + y * 4 + x, c)

    def slots(self, n):
        self.n_slots += n
        assert self.n_slots <= N_REMOTE
        return self.n_slots - n

    def local_slots(self, n):
        self.n_local += n
        assert self.n_local <= N_LOCAL
        return self.n_local - n

    def local(self, src, dst, slot):
        return pltpu.make_async_copy(src, dst, self.lsem.at[slot])

    def remote(self, src, dst, dev, slot):
        return pltpu.make_async_remote_copy(src_ref=src, dst_ref=dst, send_sem=self.ssem.at[slot], recv_sem=self.rsem.at[slot], device_id=dev, device_id_type=MESH)

    def barrier(self):
        sem = pltpu.get_barrier_semaphore()
        z, y, x, c = self.z, self.y, self.x, self.c
        peers = [self.partner]
        for dz in range(1, 4):
            peers.append(self.dev((z + dz) % 4, y, x, c))
            peers.append(self.dev((z + dz) % 4, y, x, 1 - c))
        peers += [self.ring1[1], self.ring1[2], self.ring2[1], self.ring2[2]]
        for peer in peers:
            pl.semaphore_signal(sem, inc=1, device_id=peer, device_id_type=MESH)
        pl.semaphore_wait(sem, len(peers))


class Gather:
    def __init__(self, place, ring, at, base):
        self.pl, self.at, self.base = place, at, base
        self.me, self.plus, self.minus = ring

    def copy(self, i):
        me = self.me
        before, after = (me + 3) % 4, (me + 1) % 4
        j, h, dev = (
            (me, 0, self.plus), (me, 1, self.minus), (me, 1, self.plus), (me, 0, self.minus), (before, 0, self.plus), (after, 1, self.minus),
        )[i]
        return self.pl.remote(self.at(j, h), self.at(j, h), dev, self.base + i)

    def start(self):
        for i in range(4):
            self.copy(i).start()

    def relay(self):
        for i in range(2):
            self.copy(i).wait_recv()
            self.copy(4 + i).start()

    def near(self):
        self.copy(2).wait_recv()
        self.copy(3).wait_recv()

    def far(self):
        self.copy(4).wait_recv()
        self.copy(5).wait_recv()
        for i in range(6):
            self.copy(i).wait_send()

    def finish(self):
        self.near()
        self.far()


class Reduce:
    def __init__(self, place, ring, own, held, add, base):
        self.pl, self.own, self.held, self.add, self.base = place, own, held, add, base
        self.me, self.plus, self.minus = ring

    def copy(self, i):
        me, own, held = self.me, self.own, self.held
        far, after, before = (me + 2) % 4, (me + 1) % 4, (me + 3) % 4
        if i == 0:
            src, dst = own(far, 0), held(0).at[0]
        elif i == 1:
            src, dst = own(far, 1), held(0).at[1]
        elif i == 2:
            src, dst = own(after, 1), held(1).at[1]
        elif i == 3:
            src, dst = own(before, 0), held(2).at[0]
        elif i == 4:
            src, dst = held(0).at[0], held(1).at[0]
        else:
            src, dst = held(0).at[1], held(2).at[1]
        return self.pl.remote(src, dst, self.minus if i % 2 else self.plus, self.base + i)

    def start(self):
        for i in range(4):
            self.copy(i).start()

    def relay(self):
        for i in range(2):
            self.copy(i).wait_recv()
            self.add(i, (self.me + 3) % 4 if i else (self.me + 1) % 4)
            self.copy(4 + i).start()

    def finish(self):
        for i in range(2, 6):
            self.copy(i).wait_recv()
        for i in range(6):
            self.copy(i).wait_send()


def loop(n, body, start=0):
    def one(i, carry):
        body(i)
        return carry
    lax.fori_loop(start, n, one, 0)


def by_rows(body):
    def one(i):
        body(i // (HALF // STEP), pl.ds(pl.multiple_of(i % (HALF // STEP) * STEP, STEP), STEP))
    loop(2 * HALF // STEP, one)


def inverse_rms(rows):
    return lax.rsqrt(jnp.mean(rows * rows, axis=-1, keepdims=True) + 1e-6)


def rms(rows):
    return (rows * inverse_rms(rows)).astype(BF16)


def cotangent(h, e, dn):
    r = inverse_rms(h)
    back = r * dn - h * (r * r * r * jnp.mean(h * dn, axis=-1, keepdims=True))
    return (e + back).astype(BF16)


class Rows:
    def __init__(self, place, part, held):
        self.pl, self.part, self.held = place, part, held
        self.base = place.slots(6 * CHUNKS)

    def __call__(self, k):
        part, held = self.part, self.held

        def add(h, j):
            def one(i):
                rows = pl.ds(pl.multiple_of(i * STEP, STEP), STEP)
                held[0, k, h, rows] = held[0, k, h, rows] + part[k, j, h, rows]
            loop(HALF // STEP, one)
        return Reduce(self.pl, self.pl.z_ring, lambda j, h: part.at[k, j, h], lambda b: held.at[b, k], add, self.base + 6 * k)

    def total(self, k, h, rows):
        return self.part[k, self.pl.z, h, rows] + self.held[1, k, h, rows] + self.held[2, k, h, rows]


class Spreads:
    def __init__(self, place, ref):
        self.pl, self.ref = place, ref
        self.base = place.slots(6 * CHUNKS)

    def __call__(self, k):
        return Gather(self.pl, self.pl.z_ring, lambda j, h: self.ref.at[k, j, h], self.base + 6 * k)


class Weights:
    def __init__(self, place, s, shards, held, outs):
        self.pl, self.s, self.shards, self.held, self.outs = place, s, shards, held, outs
        self.slots = place.slots(8)
        self.out_slot = place.slots(1)
        self.swap_slots = place.slots(3)
        self.local = place.local_slots(3)
        self.copy_local = place.local_slots(3)
        self.first = Gather(place, place.ring2, lambda j, h: held.at[place.a1, j, h], place.slots(6))
        self.second = Gather(place, place.ring1, lambda j, h: held.at[j, 2 * h:2 * h + 2], place.slots(6))

    def parts(self, dz):
        place = self.pl
        target = (place.z + dz) % 4
        core = place.z // 2
        a1, a2 = place.order(place.y, place.x, core)
        cols = pl.ds(pl.multiple_of(target * WIDE, WIDE), WIDE)
        for m in range(2):
            yield m, self.shards[m].at[:, cols], self.held.at[a1, a2, place.z % 2, m], place.dev(target, place.y, place.x, core)

    def out_part(self, core):
        a1, a2 = self.pl.order(self.pl.y, self.pl.x, core)
        return self.shards[2].at[2 * core:2 * core + 2], self.held.at[a1, a2, :, 2]

    def source(self, act_remote, act_local):
        place, s = self.pl, self.s
        mine = place.z // 2 == s

        @pl.when(place.c == s)
        def _():
            for dz in range(1, 4):
                for m, src, dst, dev in self.parts(dz):
                    act_remote(place.remote(src, dst, dev, self.slots + 2 * dz + m))

            @pl.when(mine)
            def _():
                for m, src, dst, _ in self.parts(0):
                    act_local(place.local(src, dst, self.local + m))

            @pl.when(jnp.logical_not(mine))
            def _():
                for m, src, dst, _ in self.parts(0):
                    act_remote(place.remote(src, dst, place.partner, self.slots + m))
            src, dst = self.out_part(s)
            act_local(place.local(src, dst, self.local + 2))
            src, dst = self.out_part(1 - s)
            act_remote(place.remote(src, dst, place.partner, self.out_slot))

    def send(self):
        self.source(lambda copy: copy.start(), lambda copy: copy.start())

    def arrive(self):
        place, s = self.pl, self.s
        for dz in range(4):
            source = (place.z + 4 - dz) % 4
            here = source // 2 == place.c
            if dz == 0:
                here = jnp.logical_and(here, place.c != s)

            @pl.when(here)
            def _(dz=dz, source=source):
                for m in range(2):
                    dst = self.held.at[place.a1, place.a2, source % 2, m]
                    place.remote(dst, dst, place.partner, self.slots + 2 * dz + m).wait_recv()

        self.source(lambda copy: copy.wait_send(), lambda copy: copy.wait())

        @pl.when(place.c != s)
        def _():
            _, dst = self.out_part(1 - s)
            place.remote(dst, dst, place.partner, self.out_slot).wait_recv()

    def place_of(self, m, p, core):
        if m < 2:
            return self.outs[m].at[pl.ds(2 * core, 2), p]
        return self.outs[m].at[p, pl.ds(2 * core, 2)]

    def half_of(self, m, core):
        if m < 2:
            return self.outs[m].at[pl.ds(2 * core, 2)]
        return self.outs[m].at[:, pl.ds(2 * core, 2)]

    def spread(self, a1):
        place = self.pl

        def one(a2):
            x, y = place.order(a2, a1, place.c)
            p = y * 4 + x
            for m in range(3):
                src = self.held.at[a1, a2, :, m]
                dst = self.place_of(m, p, place.c)
                place.remote(src, dst, place.partner, self.swap_slots + m).start()
                place.local(src, dst, self.copy_local + m).start()
        loop(4, one)

    def done(self):
        place = self.pl
        for m in range(3):
            mine, other = self.half_of(m, place.c), self.half_of(m, 1 - place.c)
            place.remote(mine, other, place.partner, self.swap_slots + m).wait_recv()
            place.remote(mine, other, place.partner, self.swap_slots + m).wait_send()
            place.local(mine, mine, self.copy_local + m).wait()

    def step1(self):
        self.arrive()
        self.first.start()

    def step2(self):
        self.first.relay()

    def step3(self):
        self.first.finish()
        self.second.start()
        self.spread(self.pl.a1)

    def step4(self):
        self.second.relay()

    def step5(self):
        self.second.near()
        self.spread((self.pl.a1 + 3) % 4)
        self.spread((self.pl.a1 + 1) % 4)

    def step6(self):
        self.second.far()
        self.spread((self.pl.a1 + 2) % 4)


class Grads:
    def __init__(self, place, s, m, part, bufs, out):
        self.pl, self.s, self.m, self.part, self.out = place, s, m, part, out
        mine, held1, sum1, held2, sum2 = (buf.at[m] for buf in bufs)
        self.mine, self.held1, self.sum1, self.held2, self.sum2 = mine, held1, sum1, held2, sum2
        self.swap_slot = place.slots(1)
        self.hand_slots = place.slots(4)
        self.local = place.local_slots(1)

        def add1(h, j):
            def one(i):
                k, q = i // 2, i % 2
                held1[0, h, k, q] = held1[0, h, k, q] + mine[j, 2 * h + k, q]
            loop(4, one)
        self.first = Reduce(place, place.ring1, lambda j, h: mine.at[j, 2 * h:2 * h + 2], lambda b: held1.at[b], add1, place.slots(6))

        def add2(h, j):
            held2[0, h] = held2[0, h] + sum1[j, h]
        self.second = Reduce(place, place.ring2, lambda j, h: sum1.at[j, h], lambda b: held2.at[b], add2, place.slots(6))

    def part_of(self, p, core):
        if self.m < 2:
            return self.part.at[pl.ds(2 * core, 2), p]
        return self.part.at[p, pl.ds(2 * core, 2)]

    def swap(self):
        place = self.pl

        def one(p):
            other = 1 - place.c
            a1, a2 = place.order(p // 4, p % 4, other)
            place.remote(self.part_of(p, other), self.mine.at[a1, a2], place.partner, self.swap_slot).start()
        loop(16, one)

    def combine(self):
        place, mine = self.pl, self.mine
        whole = place.remote(mine, mine, place.partner, self.swap_slot)
        whole.wait_recv()

        def one(p):
            a1, a2 = place.order(p // 4, p % 4, place.c)
            for q in range(2):
                own = self.part[2 * place.c + q, p] if self.m < 2 else self.part[p, 2 * place.c + q]
                mine[a1, a2, q] = mine[a1, a2, q] + own
        loop(16, one)
        self.first.start()
        whole.wait_send()

    def turn(self):
        place, mine, held1, sum1 = self.pl, self.mine, self.held1, self.sum1
        self.first.finish()

        def one(i):
            h, k, q = i // 4, i // 2 % 2, i % 2
            sum1[i // 2, q] = mine[place.a1, i // 2, q] + held1[1, h, k, q] + held1[2, h, k, q]
        loop(8, one)
        self.second.start()

    def last(self):
        place = self.pl
        self.second.finish()
        for h in range(2):
            self.sum2[h] = self.sum1[place.a2, h] + self.held2[1, h] + self.held2[2, h]
        self.hand(False)

    def shard(self, source):
        return self.out.at[:, pl.ds(pl.multiple_of(source * WIDE, WIDE), WIDE)]

    def hand(self, wait):
        place, s = self.pl, self.s
        to_self = place.c == s

        def stay(src, dst):
            copy = place.local(src, dst, self.local)
            copy.wait() if wait else copy.start()

        def go(src, dst, dev, slot):
            copy = place.remote(src, dst, dev, slot)
            copy.wait_send() if wait else copy.start()

        if self.m == 2:
            rows = self.out.at[pl.ds(2 * place.c, 2)]
            pl.when(to_self)(lambda: stay(self.sum2, rows))
            pl.when(jnp.logical_not(to_self))(lambda: go(self.sum2, rows, place.partner, self.hand_slots))
            return
        for dz in range(4):
            target = (place.z + dz) % 4
            src, dst = self.sum2.at[target % 2], self.shard(place.z)
            here = target // 2 == place.c
            send = functools.partial(go, src, dst, place.dev(target, place.y, place.x, s), self.hand_slots + dz)
            if dz:
                pl.when(here)(send)
            else:
                pl.when(jnp.logical_and(here, to_self))(functools.partial(stay, src, dst))
                pl.when(jnp.logical_and(here, jnp.logical_not(to_self)))(send)

    def done(self):
        place, s = self.pl, self.s

        def land(dst, slot):
            place.remote(dst, dst, place.partner, slot).wait_recv()

        @pl.when(place.c == s)
        def _():
            if self.m == 2:
                land(self.out.at[pl.ds(2 * (1 - place.c), 2)], self.hand_slots)
                return
            for dz in range(1, 4):
                land(self.shard((place.z + 4 - dz) % 4), self.hand_slots + dz)
            pl.when(place.z // 2 != s)(lambda: land(self.shard(place.z), self.hand_slots))
        self.hand(True)


def mm(a, b):
    return jnp.dot(a, b, preferred_element_type=F32)


def mm_nt(a, b):
    return lax.dot_general(a, b, (((1,), (1,)), ((), ())), preferred_element_type=F32)


def mm_tn(a, b):
    return lax.dot_general(a, b, (((0,), (0,)), ((), ())), preferred_element_type=F32)


def at_cols(i):
    return pl.ds(pl.multiple_of(i * COLS, COLS), COLS)


def chunk(ref, k):
    return ref[k].reshape(ROWS, WIDE)


def pre_acts(n_ref, k, gate, inn, a_ref, b_ref, slot):
    def one(i):
        cols = at_cols(i)
        n = chunk(n_ref, k)
        a_ref[slot, :, cols] = mm(n, gate[:, :, :, cols].reshape(WIDE, COLS))
        b_ref[slot, :, cols] = mm(n, inn[:, :, :, cols].reshape(WIDE, COLS))
    loop(WIDE // COLS, one)


def hidden(a_ref, b_ref, slot, u_ref, k):
    def one(i):
        rows = pl.ds(pl.multiple_of(i * STEP, STEP), STEP)
        a = a_ref[slot, rows]
        u_ref[k, rows] = (a * jax.nn.sigmoid(a) * b_ref[slot, rows]).astype(BF16)
    loop(ROWS // STEP, one)


def project(u_ref, k, out, part):
    def one(i):
        cols = at_cols(i)
        o = mm(u_ref[k], out[:, :, :, cols].reshape(WIDE, COLS))
        part[k, :, :, :, cols] = o.reshape(4, 2, HALF, COLS)
    loop(WIDE // COLS, one)


def hidden_back(e_ref, k, out, t_ref, a_ref, b_ref, slot, da_ref, db_ref):
    def dot(i):
        t_ref[:, at_cols(i)] = mm_nt(chunk(e_ref, k), out[pl.ds(8 * i, 8)].reshape(COLS, WIDE))
    loop(WIDE // COLS, dot)

    def one(i):
        rows = pl.ds(pl.multiple_of(i * STEP, STEP), STEP)
        t, a, b = t_ref[rows], a_ref[slot, rows], b_ref[slot, rows]
        s = jax.nn.sigmoid(a)
        da_ref[k, rows] = (t * b * s * (1.0 + a * (1.0 - s))).astype(BF16)
        db_ref[k, rows] = (t * a * s).astype(BF16)
    loop(ROWS // STEP, one)


def input_back(da_ref, db_ref, k, gate, inn, part):
    def one(i):
        dn = mm_nt(da_ref[k], gate[pl.ds(2 * i, 2)].reshape(COLS, WIDE)) + mm_nt(db_ref[k], inn[pl.ds(2 * i, 2)].reshape(COLS, WIDE))
        part[k, :, :, :, at_cols(i)] = dn.reshape(4, 2, HALF, COLS)
    loop(WIDE // COLS, one)


def weight_grad(lhs, rhs, out, m):
    def one(i):
        cols = pl.ds(pl.multiple_of(i * 256, 256), 256)
        left = lhs[..., cols].reshape(CHUNKS * ROWS, 256)
        d = mm_tn(left, rhs[...].reshape(CHUNKS * ROWS, WIDE))
        if m < 2:
            out[i] = d.reshape(16, 16, WIDE)
        else:
            out[pl.ds(4 * i, 4)] = d.reshape(4, 4, 16, WIDE)
    loop(4, one)


def kernel_1(x_ref, g_ref, wg, wi, wo, ga_ref, h_ref, n1_ref, n0_out, a_out, b_out, u_out, v1g, v1i, v1o,
             n0, a_s, b_s, u_s, part, held, w0g, w0i, w0o, held_w, held_w1, ssem, rsem, lsem):
    place = Place(ssem, rsem, lsem)
    z, c = place.z, place.c
    shards = (wg, wi, wo)
    w0 = Weights(place, 0, shards, held_w, (w0g, w0i, w0o))
    w1 = Weights(place, 1, shards, held_w1, (v1g, v1i, v1o))
    rows_n0, rows_g, rows_o, rows_n1 = Spreads(place, n0), Spreads(place, ga_ref), Rows(place, part, held), Spreads(place, n1_ref)
    g_copy = place.local(g_ref.at[c], ga_ref.at[:, z], place.local_slots(1))
    save = place.local_slots(4)

    def saves(k):
        return (
            place.local(a_s.at[k], a_out.at[k], save + 0), place.local(b_s.at[k], b_out.at[k], save + 1), place.local(u_s.at[k], u_out.at[k], save + 2),
        )
    n0_save = place.local(n0, n0_out, save + 3)

    place.barrier()
    w0.send()
    g_copy.start()

    def start_n0(k):
        def norm(h, rows):
            n0[k, z, h, rows] = rms(x_ref[c, k, h, rows].astype(F32))
        by_rows(norm)
        rows_n0(k).start()
    loop(CHUNKS, start_n0)
    w0.step1()
    rows_n0(0).relay()
    w0.step2()
    loop(CHUNKS, lambda k: rows_n0(k).relay(), 1)
    w0.step3()
    g_copy.wait()
    loop(CHUNKS, lambda k: rows_n0(k).finish())
    n0_save.start()
    loop(CHUNKS, lambda k: rows_g(k).start())
    w0.step4()
    w1.send()
    w0.step5()
    loop(CHUNKS, lambda k: rows_g(k).relay())
    w0.step6()
    w1.step1()
    w0.done()

    def pipeline(i):
        @pl.when(i < CHUNKS)
        def _():
            @pl.when(i >= 1)
            def _():
                for copy in saves(i - 1):
                    copy.wait()
            pre_acts(n0, i, w0g, w0i, a_s, b_s, i)
            hidden(a_s, b_s, i, u_s, i)
            for copy in saves(i):
                copy.start()
            project(u_s, i, w0o, part)
            rows_o(i).start()
        pl.when(jnp.logical_and(i >= 1, i <= CHUNKS))(lambda: rows_o(i - 1).relay())
        pl.when(i == 0)(lambda: w1.step2())
        pl.when(i == 1)(lambda: w1.step3())
        pl.when(i == 2)(lambda: w1.step4())
        pl.when(i == 3)(lambda: w1.step5())
        pl.when(i == 4)(lambda: w1.step6())

        @pl.when(jnp.logical_and(i >= 2, i <= CHUNKS + 1))
        def _():
            k = i - 2
            rows_o(k).finish()

            def step(h, rows):
                o = rows_o.total(k, h, rows).astype(BF16).astype(F32)
                out = (x_ref[c, k, h, rows].astype(F32) + o).astype(BF16)
                h_ref[k, h, rows] = out
                n1_ref[k, z, h, rows] = rms(out.astype(F32))
            by_rows(step)
            rows_n1(k).start()
        pl.when(i >= 3)(lambda: rows_n1(i - 3).relay())
    loop(CHUNKS + 3, pipeline)
    for copy in saves(CHUNKS - 1):
        copy.wait()
    n0_save.wait()
    loop(CHUNKS, lambda k: rows_g(k).finish())
    w1.done()
    loop(CHUNKS, lambda k: rows_n1(k).finish())


def three_grads(place, s, parts, bufs, outs):
    return [Grads(place, s, m, parts[m], bufs, outs[m]) for m in range(3)]


def kernel_2(n1, ga, h_ref, v1g, v1i, v1o, wg, wi, wo, e_ref, eo_ref, v0g, v0i, v0o, gg, gi, go,
             w1g, w1i, w1o, a_s, b_s, t_s, u_s, da_s, db_s, part, held, held_w, dg, di, do, mine, held1, sum1, held2, sum2, ssem, rsem, lsem):
    place = Place(ssem, rsem, lsem)
    z = place.z
    load = place.local_slots(3)
    loads = [place.local(v, w, load + m) for m, (v, w) in enumerate(((v1g, w1g), (v1i, w1i), (v1o, w1o)))]
    for copy in loads:
        copy.start()
    w0 = Weights(place, 0, (wg, wi, wo), held_w, (v0g, v0i, v0o))
    rows_d, rows_e = Rows(place, part, held), Spreads(place, e_ref)
    gate, inn, out = three_grads(place, 1, (dg, di, do), (mine, held1, sum1, held2, sum2), (gg, gi, go))
    place.barrier()
    w0.send()
    for copy in loads:
        copy.wait()

    def ahead(k):
        pre_acts(n1, k, w1g, w1i, a_s, b_s, k % 2)
        hidden(a_s, b_s, k % 2, u_s, k)

    def back(k):
        hidden_back(ga, k, w1o, t_s, a_s, b_s, k % 2, da_s, db_s)
        input_back(da_s, db_s, k, w1g, w1i, part)
        rows_d(k).start()

    def close(k):
        rows_d(k).finish()

        def step(h, rows):
            dn = rows_d.total(k, h, rows)
            e = cotangent(h_ref[k, h, rows].astype(F32), ga[k, z, h, rows].astype(F32), dn)
            e_ref[k, z, h, rows] = e
            eo_ref[k, h, rows] = e
        by_rows(step)
        rows_e(k).start()

    def early(k):
        ahead(k)
        back(k)
        pl.when(k == 0)(w0.step1)
        pl.when(k == 1)(w0.step2)
    loop(2, early)
    rows_d(0).relay()
    w0.step3()

    def middle(k):
        ahead(k)
        pl.when(k == 2)(w0.step4)
    loop(4, middle, 2)
    rows_d(1).relay()
    weight_grad(u_s, ga, do, 2)
    out.swap()
    w0.step5()

    def late(k):
        back(k)
        close(k - 2)
        pl.when(k == 2)(w0.step6)
    loop(4, late, 2)
    out.combine()
    rows_d(2).relay()
    weight_grad(n1, da_s, dg, 0)
    gate.swap()
    rows_d(3).relay()
    rows_e(0).relay()
    rows_e(1).relay()
    weight_grad(n1, db_s, di, 1)
    inn.swap()
    close(2)
    out.first.relay()
    gate.combine()
    close(3)
    inn.combine()
    rows_e(2).relay()
    out.turn()
    gate.first.relay()
    rows_e(3).relay()
    out.second.relay()
    inn.first.relay()
    out.last()
    gate.turn()
    w0.done()
    gate.second.relay()
    inn.turn()
    gate.last()
    inn.second.relay()
    loop(CHUNKS, lambda k: rows_e(k).finish())
    inn.last()
    out.done()
    gate.done()
    inn.done()


def kernel_3(e_ref, x_ref, eo_ref, n0_in, a_in, b_in, u_in, v0g, v0i, v0o, dx_ref, gg, gi, go,
             w0g, w0i, w0o, n0, a_s, b_s, t_s, u_s, da_s, db_s, part, held, dg, di, do, mine, held1, sum1, held2, sum2, ssem, rsem, lsem):
    place = Place(ssem, rsem, lsem)
    c = place.c
    load = place.local_slots(5)
    loads = [place.local(v, w, load + m) for m, (v, w) in enumerate(((v0o, w0o), (v0g, w0g), (v0i, w0i), (u_in, u_s), (n0_in, n0)))]
    load_ab = place.local_slots(4)

    def loads_ab(k):
        return place.local(a_in.at[k], a_s.at[k % 2], load_ab + 2 * (k % 2)), place.local(b_in.at[k], b_s.at[k % 2], load_ab + 2 * (k % 2) + 1)
    loads[0].start()
    for copy in loads_ab(0):
        copy.start()
    loads[1].start()
    loads[2].start()
    for copy in loads_ab(1):
        copy.start()
    loads[3].start()
    loads[4].start()
    rows_d = Rows(place, part, held)
    gate, inn, out = three_grads(place, 0, (dg, di, do), (mine, held1, sum1, held2, sum2), (gg, gi, go))
    swap = place.remote(dx_ref.at[c], dx_ref.at[c], place.partner, place.slots(1))
    place.barrier()
    for copy in loads[:3]:
        copy.wait()

    def hide(k):
        for copy in loads_ab(k):
            copy.wait()
        hidden_back(e_ref, k, w0o, t_s, a_s, b_s, k % 2, da_s, db_s)

    def close(k):
        rows_d(k).finish()

        def step(h, rows):
            dn = rows_d.total(k, h, rows)
            dx_ref[c, k, h, rows] = cotangent(x_ref[c, k, h, rows].astype(F32), eo_ref[k, h, rows].astype(F32), dn)
        by_rows(step)

    def early(k):
        hide(k)
        for copy in loads_ab(k + 2):
            copy.start()
        input_back(da_s, db_s, k, w0g, w0i, part)
        rows_d(k).start()
    loop(2, early)
    loads[3].wait()
    weight_grad(u_s, e_ref, do, 2)
    out.swap()
    rows_d(0).relay()
    loop(4, hide, 2)
    loads[4].wait()
    out.combine()
    rows_d(1).relay()
    weight_grad(n0, da_s, dg, 0)
    gate.swap()

    def late(k):
        input_back(da_s, db_s, k, w0g, w0i, part)
        rows_d(k).start()
        close(k - 2)
    loop(4, late, 2)
    gate.combine()
    weight_grad(n0, db_s, di, 1)
    inn.swap()
    rows_d(2).relay()
    out.first.relay()
    rows_d(3).relay()
    inn.combine()
    gate.first.relay()
    out.turn()
    close(2)
    inn.first.relay()
    out.second.relay()
    gate.turn()
    out.last()
    close(3)
    swap.start()
    gate.second.relay()
    inn.turn()
    gate.last()
    inn.second.relay()
    inn.last()
    swap.wait()
    out.done()
    gate.done()
    inn.done()


VM = pl.BlockSpec(memory_space=pltpu.VMEM)
ANY = pl.BlockSpec(memory_space=pl.ANY)


def sds(shape, dtype):
    return jax.ShapeDtypeStruct(shape, dtype)


ALL_ROWS = (CHUNKS, 4, 2, HALF, WIDE)
OWN_ROWS = (CHUNKS, 2, HALF, WIDE)
FLAT_ROWS = (CHUNKS, ROWS, WIDE)
UP = (4, 16, 16, WIDE)
DOWN = (16, 4, 16, WIDE)
W_SHAPES = [sds(UP, BF16), sds(UP, BF16), sds(DOWN, BF16)]
G_SHAPES = [sds((16, 4 * WIDE), F32), sds((16, 4 * WIDE), F32), sds((4, 16, WIDE), F32)]
ROW_BUFS = [pltpu.VMEM(ALL_ROWS, F32), pltpu.VMEM((3,) + OWN_ROWS, F32)]
W_FULL = [pltpu.VMEM(UP, BF16), pltpu.VMEM(UP, BF16), pltpu.VMEM(DOWN, BF16)]
W_HELD = pltpu.VMEM((4, 4, 2, 3, 16, WIDE), BF16)
BACK_BUFS = [pltpu.VMEM((2, ROWS, WIDE), F32)] * 2 + [pltpu.VMEM((ROWS, WIDE), F32)] + [pltpu.VMEM(FLAT_ROWS, BF16)] * 3
G_BUFS = [
    pltpu.VMEM(UP, F32),
    pltpu.VMEM(UP, F32),
    pltpu.VMEM(DOWN, F32),
    pltpu.VMEM((3, 4, 4, 2, 16, WIDE), F32),
    pltpu.VMEM((3, 3, 2, 2, 2, 16, WIDE), F32),
    pltpu.VMEM((3, 4, 2, 16, WIDE), F32),
    pltpu.VMEM((3, 3, 2, 16, WIDE), F32),
    pltpu.VMEM((3, 2, 16, WIDE), F32),
]
SEMS = [pltpu.SemaphoreType.DMA((N_REMOTE,)), pltpu.SemaphoreType.DMA((N_REMOTE,)), pltpu.SemaphoreType.DMA((N_LOCAL,))]


def call(kernel, cid, ins, outs, out_specs, scratch):
    return pl.pallas_call(
        kernel,
        out_shape=outs,
        in_specs=ins,
        out_specs=out_specs,
        scratch_shapes=scratch + SEMS,
        compiler_params=pltpu.CompilerParams(collective_id=cid, has_side_effects=True, vmem_limit_bytes=67043328),
        name=kernel.__name__,
    )


def solution(mesh):
    act_spec = P(None, 'data', None, None)
    weight_spec = P('stage', None, 'data', None)

    def per_device(x, g, w_gate, w_in, w_out):
        xs = x.reshape((2,) + OWN_ROWS)
        gs = g.reshape((2,) + OWN_ROWS)
        shards = (w_gate.reshape(16, 4 * WIDE), w_in.reshape(16, 4 * WIDE), w_out.reshape(4, 16, WIDE))

        outs = [sds(ALL_ROWS, BF16), sds(OWN_ROWS, BF16), sds(ALL_ROWS, BF16)]
        outs += [sds(ALL_ROWS, BF16), sds(FLAT_ROWS, F32), sds(FLAT_ROWS, F32), sds(FLAT_ROWS, BF16)] + W_SHAPES
        scratch = [pltpu.VMEM(ALL_ROWS, BF16), pltpu.VMEM(FLAT_ROWS, F32), pltpu.VMEM(FLAT_ROWS, F32), pltpu.VMEM(FLAT_ROWS, BF16)]
        scratch += ROW_BUFS + W_FULL + [W_HELD] * 2
        g_all, h1, n1, n0, a0, b0, u0, *w1 = call(kernel_1, 1, [VM] * 5, outs, [VM] * 3 + [ANY] * 7, scratch)(xs, gs, *shards)

        outs = [sds(ALL_ROWS, BF16), sds(OWN_ROWS, BF16)] + W_SHAPES + G_SHAPES
        scratch = W_FULL + BACK_BUFS + ROW_BUFS + [W_HELD] + G_BUFS
        e_all, e_own, *rest = call(kernel_2, 2, [VM] * 3 + [ANY] * 3 + [VM] * 3, outs, [VM] * 2 + [ANY] * 3 + [VM] * 3, scratch)(n1, g_all, h1, *w1, *shards)
        w0, own1 = rest[:3], rest[3:]

        outs = [sds((2,) + OWN_ROWS, BF16)] + G_SHAPES
        scratch = W_FULL + [pltpu.VMEM(ALL_ROWS, BF16)] + BACK_BUFS + ROW_BUFS + G_BUFS
        dx, *own0 = call(kernel_3, 3, [VM] * 3 + [ANY] * 7, outs, [VM] * 4, scratch)(e_all, xs, e_own, n0, a0, b0, u0, *w0)
        first = lax.axis_index('stage') == 0
        own = [jnp.where(first, s0, s1) for s0, s1 in zip(own0, own1)]
        return (dx.reshape(x.shape), own[0].reshape(w_gate.shape), own[1].reshape(w_in.shape), own[2].reshape(w_out.shape))

    return jax.shard_map(per_device, mesh=mesh, in_specs=(act_spec, act_spec, weight_spec, weight_spec, weight_spec), out_specs=(act_spec, weight_spec, weight_spec, weight_spec), check_vma=False)
```

time: 2510 us -> 285 us (0.11)
  waiting for transfers between devices: 1770 us -> 0 us
  matrix products: 583 us -> 0 us
  Pallas kernels: 0 us -> 280 us
  starting transfers between devices: 46 us -> 0 us
  local copies, waits for them, and re-layouts: 44 us -> 0.97 us
  other arithmetic: 43.2 us -> 3.65 us
    reduce_scatter x3 -> x0, waiting for transfers between devices: 1170 us -> none  [the longest x1 394 us: per_device(): lax.psum_scatter(jnp.stack(grad_sums[2]), 'data', scatter_dimension=1, ti...]
    dot_general x80 -> x0, matrix products: 583 us -> none  [the longest x8 161 us: layer_bwd(): jnp.einsum('td,tf->df', normed, d_gate, preferred_element_type=jnp.float32)]
    all_gather x6 -> x0, waiting for transfers between devices: 480 us -> none  [the longest x1 82 us: per_device(): gate_full = lax.all_gather(w_gate[0], 'data', axis=1, tiled=True)]
    pallas_call x0 -> x3, Pallas kernels: none -> 280 us  [the longest x1 105 us: per_device(): call(kernel_1, 1, [VM] * 5, outs, [VM] * 3 + [ANY] * 7, scratch)]
    ppermute x18 -> x0, waiting for transfers between devices: 86.8 us -> none  [the longest x9 78.2 us: bwd_tick(): sent_out = lax.ppermute(d_in, 'stage', bwd_pairs)]
    ppermute x18 -> x0, starting transfers between devices: 45.6 us -> none  [the longest x9 34 us: fwd_tick(): sent_out = lax.ppermute(block_out, 'stage', fwd_pairs)]
  transfers between devices with their start and end apart: 28 -> 0, of which waited for: 28 -> 0; matrix products, arithmetic and copies ran while one was open for 0% -> 0% of each run, Pallas kernels for 0% -> 0%
where the time goes in v2:
time: 285 us
  Pallas kernels  280 us (98%)
  other arithmetic  3.65 us (1%)
    pallas_call x1, Pallas kernels, per_device(): call(kernel_1, 1, [VM] * 5, outs, [VM] * 3 + [ANY] * 7, scratch)  105 us
    pallas_call x1, Pallas kernels, per_device(): call(kernel_2, 2, [VM] * 3 + [ANY] * 3 + [VM] * 3, outs, [VM] * 2 + [ANY]...  102 us
    pallas_call x1, Pallas kernels, per_device(): call(kernel_3, 3, [VM] * 3 + [ANY] * 7, outs, [VM] * 4, scratch)  72.9 us

profile of v2, /device:TPU:0, one launch (start us, length us, event | category | flops | bytes accessed | tf_op | source)
XLA Modules:
  0.0 285.2 jit_solution(17462740451540250214)
XLA Ops:
  0.6 104.9 %kernel_1.1 = (bf16[4,4,2,32,1024]{4,3,2,1,0:T(8,128)(2,1)}, bf16[4,2,32,1024]{3,2,1,0:T(8,128)(2,1)}, bf16[4,4,2,32,1024]{4,3,2,1,0:T(8,128)(2,1)}, bf16[4,4,2,...) custom-call(bf16[2,4,2,32,1024]{4,3,2,1,0:T(8,128)(2,1)} %bitcast.11, ...), custom_call_target="tpu_custom_call" | custom-call | tf_op jit(solution)/shard_map/kernel_1/pallas_call | solution.py:856
  105.5 102.1 %kernel_2.1 = (bf16[4,4,2,32,1024]{4,3,2,1,0:T(8,128)(2,1)}, bf16[4,2,32,1024]{3,2,1,0:T(8,128)(2,1)}, bf16[4,16,16,1024]{3,2,1,0:T(8,128)(2,1)}, bf16[4,16,16,1...) custom-call(bf16[4,4,2,32,1024]{4,3,2,1,0:T(8,128)(2,1)} %get-tuple-, ...), custom_call_target="tpu_custom_call" | custom-call | tf_op jit(solution)/shard_map/kernel_2/pallas_call | solution.py:860
  207.7 72.9 %kernel_3.1 = (bf16[2,4,2,32,1024]{4,3,2,1,0:T(8,128)(2,1)}, f32[16,4096]{1,0:T(8,128)}, f32[16,4096]{1,0:T(8,128)}, f32[4,16,1024]{2,1,0:T(8,128)}) custom-call(bf16[4,4,2,32,1024]{4,3,2,1,0:T(8,128)(2,1)} %get-tuple-element.32.e_ref, bf16[2,4,2,32,1024]{4,3,2,1,0:T(8,128)(2,1)} %bitcast.12, bf16[4,2,32,1024]{3,2,1,0:T(8,128)(2,1)} %get-tuple-element.33.eo_ref, ...), custom_call_target="tpu_custom_call" | custom-call | tf_op jit(solution)/shard_map/kernel_3/pallas_call | solution.py:865
  280.6 0.0 copy-start
  280.6 1.8 broadcast_select_fusion
  282.4 1.9 select_bitcast_fusion
  284.2 0.0 copy-done
  284.2 1.0 copy.10
Async XLA Ops:
  280.6 3.7 %copy-start = (bf16[2,4,2,32,1024]{4,3,2,1,0:T(8,128)(2,1)S(1)}, bf16[2,4,2,32,1024]{4,3,2,1,0:T(8,128)(2,1)}, u32[]{:S(2)}) copy-start(bf16[2,4,2,32,1024]{4,3,2,1,0:T(8,128)(2,1)} %get-tuple-element.41) | copy-start | bytes 3145732

commit v3 on v0

v3 whole, which is shorter than its diff:
```python
import functools

import jax
import jax.numpy as jnp
from jax import lax
from jax.experimental import pallas as pl
from jax.experimental.pallas import tpu as pltpu
from jax.sharding import PartitionSpec as P

MESH = pl.DeviceIdType.MESH
BF16 = jnp.bfloat16
F32 = jnp.float32
RING = 4
CHUNKS = 4
HALF = 128 // CHUNKS
ROWS = 8 * HALF
STEP = 16
COLS = 512
WIDE = 1024
N_REMOTE = 224
N_LOCAL = 40


class Place:
    def __init__(self, ssem, rsem, lsem, phase):
        d = lax.axis_index('data')
        self.c = lax.axis_index('stage')
        self.z, self.y, self.x = d // 16, (d // 4) % 4, d % 4
        self.ssem, self.rsem, self.lsem, self.phase = ssem, rsem, lsem, phase
        self.n_slots = self.n_local = 0
        self.partner = self.dev(self.z, self.y, self.x, 1 - self.c)

    @staticmethod
    def dev(z, y, x, c):
        return (z * 16 + y * 4 + x, c)

    def slots(self, n):
        self.n_slots += n
        assert self.n_slots <= N_REMOTE
        return self.n_slots - n

    def local_slots(self, n):
        self.n_local += n
        assert self.n_local <= N_LOCAL
        return self.n_local - n

    def local(self, src, dst, slot):
        return pltpu.make_async_copy(src, dst, self.lsem.at[slot])

    def remote(self, src, dst, dev, slot):
        return pltpu.make_async_remote_copy(src_ref=src, dst_ref=dst, send_sem=self.ssem.at[slot], recv_sem=self.rsem.at[slot], device_id=dev, device_id_type=MESH)

    def peers(self):
        z, y, x, c = self.z, self.y, self.x, self.c
        peers = [self.partner, self.dev(z, y, (x + 1) % 4, c), self.dev(z, y, (x + 3) % 4, c)]
        for step in range(1, 4):
            for core in (c, 1 - c):
                peers.append(self.dev((z + step) % 4, y, x, core))
                peers.append(self.dev(z, (y + step) % 4, x, core))
        return peers

    def signal(self, sem):
        for peer in self.peers():
            pl.semaphore_signal(sem, inc=1, device_id=peer, device_id_type=MESH)

    def wait(self, sem):
        pl.semaphore_wait(sem, len(self.peers()))


class Block:
    def __init__(self, place, b):
        self.b, self.c, self.x = b, place.c, place.x
        self.t, self.w = (place.z, place.y) if b == 0 else (place.y, place.z)
        t, w, x, c, k = self.t, self.w, self.x, self.c, 1 - self.c
        self.a1, self.a2 = self.order(w, x, c)
        self.rows = (t, self.dev((t + 1) % 4, w, x, c), self.dev((t + 3) % 4, w, x, c))
        self.ring1 = (self.a1, self.dev(t, (w + c) % 4, (x + k) % 4, c), self.dev(t, (w + 3 * c) % 4, (x + 3 * k) % 4, c))
        self.ring2 = (self.a2, self.dev(t, (w + k) % 4, (x + c) % 4, c), self.dev(t, (w + 3 * k) % 4, (x + 3 * c) % 4, c))

    def dev(self, t, w, x, c):
        return Place.dev(t, w, x, c) if self.b == 0 else Place.dev(w, t, x, c)

    @staticmethod
    def order(w, x, c):
        return (1 - c) * x + c * w, (1 - c) * w + c * x

    def index(self, m, w, x, q):
        return (w, x, q) if m == 2 else (q, w, x) if self.b == 0 else (w, q, x)

    def pieces(self, position):
        if self.b == 0:
            return [(pl.ds(pl.multiple_of(position * WIDE, WIDE), WIDE), pl.ds(0, WIDE))]
        return [(pl.ds(pl.multiple_of(u * WIDE + position * 256, 256), 256), pl.ds(u * 256, 256)) for u in range(4)]


def pair(core):
    return pl.ds(2 * core, 2)


class Gather:
    def __init__(self, place, ring, at, base):
        self.pl, self.at, self.base = place, at, base
        self.me, self.plus, self.minus = ring

    def copy(self, i):
        me = self.me
        before, after = (me + 3) % 4, (me + 1) % 4
        j, h, dev = (
            (me, 0, self.plus), (me, 1, self.minus), (me, 1, self.plus), (me, 0, self.minus), (before, 0, self.plus), (after, 1, self.minus),
        )[i]
        return self.pl.remote(self.at(j, h), self.at(j, h), dev, self.base + i)

    def start(self):
        for i in range(4):
            self.copy(i).start()

    def relay(self):
        for i in range(2):
            self.copy(i).wait_recv()
            self.copy(4 + i).start()

    def near(self):
        self.copy(2).wait_recv()
        self.copy(3).wait_recv()

    def far(self):
        self.copy(4).wait_recv()
        self.copy(5).wait_recv()
        for i in range(6):
            self.copy(i).wait_send()

    def finish(self):
        self.near()
        self.far()


class Reduce:
    def __init__(self, place, ring, own, held, add, base):
        self.pl, self.own, self.held, self.add, self.base = place, own, held, add, base
        self.me, self.plus, self.minus = ring

    def copy(self, i):
        me, own, held = self.me, self.own, self.held
        far, after, before = (me + 2) % 4, (me + 1) % 4, (me + 3) % 4
        if i == 0:
            src, dst = own(far, 0), held(0).at[0]
        elif i == 1:
            src, dst = own(far, 1), held(0).at[1]
        elif i == 2:
            src, dst = own(after, 1), held(1).at[1]
        elif i == 3:
            src, dst = own(before, 0), held(2).at[0]
        elif i == 4:
            src, dst = held(0).at[0], held(1).at[0]
        else:
            src, dst = held(0).at[1], held(2).at[1]
        return self.pl.remote(src, dst, self.minus if i % 2 else self.plus, self.base + i)

    def start(self):
        for i in range(4):
            self.copy(i).start()

    def relay(self):
        for i in range(2):
            self.copy(i).wait_recv()
            self.add(i, (self.me + 3) % 4 if i else (self.me + 1) % 4)
            self.copy(4 + i).start()

    def finish(self):
        for i in range(2, 6):
            self.copy(i).wait_recv()
        for i in range(6):
            self.copy(i).wait_send()


def loop(n, body, start=0):
    def one(i, carry):
        body(i)
        return carry
    lax.fori_loop(start, n, one, 0)


def by_rows(body):
    def one(i):
        body(i // (HALF // STEP), pl.ds(pl.multiple_of(i % (HALF // STEP) * STEP, STEP), STEP))
    loop(2 * HALF // STEP, one)


def inverse_rms(rows):
    return lax.rsqrt(jnp.mean(rows * rows, axis=-1, keepdims=True) + 1e-6)


def rms(rows):
    return (rows * inverse_rms(rows)).astype(BF16)


def cotangent(h, e, dn):
    r = inverse_rms(h)
    back = r * dn - h * (r * r * r * jnp.mean(h * dn, axis=-1, keepdims=True))
    return (e + back).astype(BF16)


class Rows:
    def __init__(self, place, ring, part, held, base):
        self.pl, self.ring, self.part, self.held, self.base = place, ring, part, held, base

    def __call__(self, k):
        part, held = self.part, self.held

        def add(h, j):
            def one(i):
                rows = pl.ds(pl.multiple_of(i * STEP, STEP), STEP)
                held[0, k, h, rows] = held[0, k, h, rows] + part[k, j, h, rows]
            loop(HALF // STEP, one)
        return Reduce(self.pl, self.ring, lambda j, h: part.at[k, j, h], lambda b: held.at[b, k], add, self.base + 6 * k)

    def total(self, k, h, rows):
        return self.part[k, self.ring[0], h, rows] + self.held[1, k, h, rows] + self.held[2, k, h, rows]


class Spreads:
    def __init__(self, place, ring, ref, base):
        self.pl, self.ring, self.ref, self.base = place, ring, ref, base

    def __call__(self, k):
        return Gather(self.pl, self.ring, lambda j, h: self.ref.at[k, j, h], self.base + 6 * k)


class Weights:
    def __init__(self, place, block, shards, held, outs, base, local):
        self.pl, self.bk, self.s, self.shards, self.held, self.outs = place, block, block.b, shards, held, outs
        self.slots, self.out_slot, self.swap_slots = base, base + 8, base + 9
        self.local, self.copy_local = local, local + 3
        self.first = Gather(place, block.ring2, lambda j, h: held.at[block.a1, j, h], base + 12)
        self.second = Gather(place, block.ring1, lambda j, h: held.at[j, 2 * h:2 * h + 2], base + 18)

    def parts(self, dz):
        bk = self.bk
        target = (bk.t + dz) % 4
        core = bk.t // 2
        a1, a2 = bk.order(bk.w, bk.x, core)
        for m in range(2):
            whole = self.held.at[a1, a2, bk.t % 2, m]
            copies = [(self.shards[m].at[:, src], self.held.at[a1, a2, bk.t % 2, m, :, dst]) for src, dst in bk.pieces(target)]
            yield m, copies, whole, bk.dev(target, bk.w, bk.x, core)

    def out_part(self, core):
        a1, a2 = self.bk.order(self.bk.w, self.bk.x, core)
        return self.shards[2].at[2 * core:2 * core + 2], self.held.at[a1, a2, :, 2]

    def source(self, wait):
        place, s = self.pl, self.s
        mine = self.bk.t // 2 == s

        def away(copies, whole, dev, slot):
            if wait:
                place.remote(whole, whole, dev, slot).wait_send()
                return
            for src, dst in copies:
                place.remote(src, dst, dev, slot).start()

        def here(copies, whole, slot):
            if wait:
                place.local(whole, whole, slot).wait()
                return
            for src, dst in copies:
                place.local(src, dst, slot).start()

        @pl.when(place.c == s)
        def _():
            for dz in range(1, 4):
                for m, copies, whole, dev in self.parts(dz):
                    away(copies, whole, dev, self.slots + 2 * dz + m)

            @pl.when(mine)
            def _():
                for m, copies, whole, _ in self.parts(0):
                    here(copies, whole, self.local + m)

            @pl.when(jnp.logical_not(mine))
            def _():
                for m, copies, whole, _ in self.parts(0):
                    away(copies, whole, place.partner, self.slots + m)
            src, dst = self.out_part(s)
            here([(src, dst)], dst, self.local + 2)
            src, dst = self.out_part(1 - s)
            away([(src, dst)], dst, place.partner, self.out_slot)

    def send(self):
        self.source(False)

    def arrive(self):
        place, bk, s = self.pl, self.bk, self.s
        for dz in range(4):
            source = (bk.t + 4 - dz) % 4
            here = source // 2 == place.c
            if dz == 0:
                here = jnp.logical_and(here, place.c != s)

            @pl.when(here)
            def _(dz=dz, source=source):
                for m in range(2):
                    dst = self.held.at[bk.a1, bk.a2, source % 2, m]
                    place.remote(dst, dst, place.partner, self.slots + 2 * dz + m).wait_recv()

        self.source(True)

        @pl.when(place.c != s)
        def _():
            _, dst = self.out_part(1 - s)
            place.remote(dst, dst, place.partner, self.out_slot).wait_recv()

    def spread(self, a1):
        place, bk = self.pl, self.bk

        def one(a2):
            x, w = bk.order(a2, a1, place.c)
            for m in range(3):
                src = self.held.at[a1, a2, :, m]
                dst = self.outs[m].at[bk.index(m, w, x, pair(place.c))]
                place.remote(src, dst, place.partner, self.swap_slots + m).start()
                place.local(src, dst, self.copy_local + m).start()
        loop(4, one)

    def done(self):
        place, bk = self.pl, self.bk
        every = slice(None)
        for m in range(3):
            mine, other = (self.outs[m].at[bk.index(m, every, every, pair(core))] for core in (place.c, 1 - place.c))
            place.remote(mine, other, place.partner, self.swap_slots + m).wait_recv()
            place.remote(mine, other, place.partner, self.swap_slots + m).wait_send()
            place.local(mine, mine, self.copy_local + m).wait()

    def step1(self):
        self.arrive()
        self.first.start()

    def step2(self):
        self.first.relay()

    def step3(self):
        self.first.finish()
        self.second.start()
        self.spread(self.bk.a1)

    def step4(self):
        self.second.relay()

    def step5(self):
        self.second.near()
        self.spread((self.bk.a1 + 3) % 4)
        self.spread((self.bk.a1 + 1) % 4)

    def step6(self):
        self.second.far()
        self.spread((self.bk.a1 + 2) % 4)


class Grads:
    def __init__(self, place, block, m, part, bufs, out, base, local):
        self.pl, self.bk, self.s, self.m, self.part, self.out = place, block, block.b, m, part, out
        mine, held1, sum1, held2, sum2 = (buf.at[m] for buf in bufs)
        self.mine, self.held1, self.sum1, self.held2, self.sum2 = mine, held1, sum1, held2, sum2
        base, self.local = base + 17 * m, local + m
        self.swap_slot, self.hand_slots = base, base + 1

        def add1(h, j):
            def one(i):
                k, q = i // 2, i % 2
                held1[0, h, k, q] = held1[0, h, k, q] + mine[j, 2 * h + k, q]
            loop(4, one)
        self.first = Reduce(place, block.ring1, lambda j, h: mine.at[j, 2 * h:2 * h + 2], lambda b: held1.at[b], add1, base + 5)

        def add2(h, j):
            held2[0, h] = held2[0, h] + sum1[j, h]
        self.second = Reduce(place, block.ring2, lambda j, h: sum1.at[j, h], lambda b: held2.at[b], add2, base + 11)

    def swap(self):
        place, bk = self.pl, self.bk

        def one(p):
            w, x, other = p // 4, p % 4, 1 - place.c
            a1, a2 = bk.order(w, x, other)
            src = self.part.at[bk.index(self.m, w, x, pair(other))]
            place.remote(src, self.mine.at[a1, a2], place.partner, self.swap_slot).start()
        loop(16, one)

    def combine(self):
        place, bk, mine = self.pl, self.bk, self.mine
        whole = place.remote(mine, mine, place.partner, self.swap_slot)
        whole.wait_recv()

        def one(p):
            w, x = p // 4, p % 4
            a1, a2 = bk.order(w, x, place.c)
            for q in range(2):
                mine[a1, a2, q] = mine[a1, a2, q] + self.part[bk.index(self.m, w, x, 2 * place.c + q)]
        loop(16, one)
        self.first.start()
        whole.wait_send()

    def turn(self):
        bk, mine, held1, sum1 = self.bk, self.mine, self.held1, self.sum1
        self.first.finish()

        def one(i):
            h, k, q = i // 4, i // 2 % 2, i % 2
            sum1[i // 2, q] = mine[bk.a1, i // 2, q] + held1[1, h, k, q] + held1[2, h, k, q]
        loop(8, one)
        self.second.start()

    def last(self):
        self.second.finish()
        for h in range(2):
            self.sum2[h] = self.sum1[self.bk.a2, h] + self.held2[1, h] + self.held2[2, h]
        self.hand(False)

    def hand(self, wait):
        place, bk, s = self.pl, self.bk, self.s
        to_self = place.c == s

        def stay(copies, whole):
            if wait:
                place.local(whole, whole, self.local).wait()
                return
            for src, dst in copies:
                place.local(src, dst, self.local).start()

        def go(copies, whole, dev, slot):
            if wait:
                place.remote(whole, whole, dev, slot).wait_send()
                return
            for src, dst in copies:
                place.remote(src, dst, dev, slot).start()

        if self.m == 2:
            copies = [(self.sum2, self.out.at[pair(place.c)])]
            pl.when(to_self)(lambda: stay(copies, self.sum2))
            pl.when(jnp.logical_not(to_self))(lambda: go(copies, self.sum2, place.partner, self.hand_slots))
            return
        for dz in range(4):
            target = (bk.t + dz) % 4
            whole = self.sum2.at[target % 2]
            copies = [(self.sum2.at[target % 2, :, own], self.out.at[:, shard]) for shard, own in bk.pieces(bk.t)]
            here = target // 2 == place.c
            send = functools.partial(go, copies, whole, bk.dev(target, bk.w, bk.x, s), self.hand_slots + dz)
            if dz:
                pl.when(here)(send)
            else:
                pl.when(jnp.logical_and(here, to_self))(functools.partial(stay, copies, whole))
                pl.when(jnp.logical_and(here, jnp.logical_not(to_self)))(send)

    def done(self):
        place, bk, s = self.pl, self.bk, self.s

        def land(like, slot):
            place.remote(like, like, place.partner, slot).wait_recv()

        @pl.when(place.c == s)
        def _():
            if self.m == 2:
                land(self.sum2, self.hand_slots)
                return
            for dz in range(1, 4):
                land(self.sum2.at[0], self.hand_slots + dz)
            pl.when(bk.t // 2 != s)(lambda: land(self.sum2.at[0], self.hand_slots))
        self.hand(True)


def mm(a, b):
    return jnp.dot(a, b, preferred_element_type=F32)


def mm_nt(a, b):
    return lax.dot_general(a, b, (((1,), (1,)), ((), ())), preferred_element_type=F32)


def mm_tn(a, b):
    return lax.dot_general(a, b, (((0,), (0,)), ((), ())), preferred_element_type=F32)


def chunk(ref, k):
    return ref[k].reshape(ROWS, WIDE)


def square(ref):
    return ref[...].reshape(WIDE, WIDE)


def pre_acts(n_ref, k, gate, inn, a_ref, b_ref, slot):
    a_ref[slot] = mm(chunk(n_ref, k), square(gate))
    b_ref[slot] = mm(chunk(n_ref, k), square(inn))


def hidden(a_ref, b_ref, slot, u_ref, k):
    def one(i):
        rows = pl.ds(pl.multiple_of(i * STEP, STEP), STEP)
        a = a_ref[slot, rows]
        u_ref[k, rows] = (a * jax.nn.sigmoid(a) * b_ref[slot, rows]).astype(BF16)
    loop(ROWS // STEP, one)


def project(u_ref, k, out, part):
    part[k] = mm(u_ref[k], square(out)).reshape(4, 2, HALF, WIDE)


def hidden_back(e_ref, k, out, t_ref, a_ref, b_ref, slot, da_ref, db_ref):
    t_ref[k] = mm_nt(chunk(e_ref, k), square(out)).reshape(4, 2, HALF, WIDE)
    per_half = HALF // STEP

    def one(i):
        rows = pl.ds(pl.multiple_of(i * STEP, STEP), STEP)
        j = i // (2 * per_half)
        h = i // per_half % 2
        t = t_ref[k, j, h, pl.ds(pl.multiple_of(i % per_half * STEP, STEP), STEP)]
        a, b = a_ref[slot, rows], b_ref[slot, rows]
        s = jax.nn.sigmoid(a)
        da_ref[k, rows] = (t * b * s * (1.0 + a * (1.0 - s))).astype(BF16)
        db_ref[k, rows] = (t * a * s).astype(BF16)
    loop(ROWS // STEP, one)


def input_back(da_ref, db_ref, k, gate, inn, part):
    def one(i):
        cols = pl.ds(pl.multiple_of(i * COLS, COLS), COLS)
        dn = mm_nt(da_ref[k], gate[pl.ds(2 * i, 2)].reshape(COLS, WIDE)) + mm_nt(db_ref[k], inn[pl.ds(2 * i, 2)].reshape(COLS, WIDE))
        part[k, :, :, :, cols] = dn.reshape(4, 2, HALF, COLS)
    loop(WIDE // COLS, one)


def weight_grad(lhs, rhs, out):
    def one(i):
        cols = pl.ds(pl.multiple_of(i * 256, 256), 256)
        left = lhs[..., cols].reshape(CHUNKS * ROWS, 256)
        out[i] = mm_tn(left, rhs[...].reshape(CHUNKS * ROWS, WIDE)).reshape(4, 4, 16, WIDE)
    loop(4, one)


def kernel(x_in, g_in, wg, wi, wo, dx_out, gg, gi, go, a_out, b_out, u_out, n_out,
           xs, hs, dxs, n0e, n1, ga, u_s, a_s, b_s, da_s, db_s, part, held, w0g, w0i, w0o, w1g, w1i, w1o, held_w,
           d_a, d_b, mine, held1, sum1, held2, sum2, ssem, rsem, lsem, phase):
    place = Place(ssem, rsem, lsem, phase)
    z, y, c = place.z, place.y, place.c
    blocks = Block(place, 0), Block(place, 1)
    per_row = 6 * CHUNKS
    z_gather, z_sum, g_gather, y_gather, y_sum = (place.slots(per_row) for _ in range(5))
    rows_n0, rows_e = (Spreads(place, blocks[0].rows, n0e, z_gather) for _ in range(2))
    rows_o, rows_d0 = (Rows(place, blocks[0].rows, part, held, z_sum) for _ in range(2))
    rows_g = Spreads(place, blocks[1].rows, ga, g_gather)
    rows_n1 = Spreads(place, blocks[1].rows, n1, y_gather)
    rows_d1 = Rows(place, blocks[1].rows, part, held, y_sum)
    shards = (wg, wi, wo)
    w0_slots, w0_local = place.slots(24), place.local_slots(6)
    w0, w0b = (Weights(place, blocks[0], shards, held_w, (w0g, w0i, w0o), w0_slots, w0_local) for _ in range(2))
    w1 = Weights(place, blocks[1], shards, held_w, (w1g, w1i, w1o), place.slots(24), place.local_slots(6))
    grad_slots, grad_local = place.slots(51), place.local_slots(3)
    bufs, outs = (mine, held1, sum1, held2, sum2), (gg, gi, go)
    (gate1, inn1, out1), (gate0, inn0, out0) = (
        [Grads(place, blocks[b], m, (d_b, d_a, d_a)[m], bufs, outs[m], grad_slots, grad_local) for m in range(3)] for b in (1, 0)
    )
    x_copy = place.local(x_in.at[c], xs, place.local_slots(1))
    g_copy = place.local(g_in.at[c], ga.at[:, y], place.local_slots(1))
    save = place.local_slots(8)
    n_save, n_load = place.local(n0e, n_out, save + 6), place.local(n_out, n1, save + 6)
    u_load = place.local(u_out, u_s, save + 7)

    def saves(k):
        slot = k % 2
        at = save + 3 * slot
        return place.local(a_s.at[slot], a_out.at[k], at), place.local(b_s.at[slot], b_out.at[k], at + 1), place.local(u_s.at[k], u_out.at[k], at + 2)

    def loads(k):
        slot = k % 2
        at = save + 3 * slot
        return place.local(a_out.at[k], a_s.at[slot], at), place.local(b_out.at[k], b_s.at[slot], at + 1)

    def start(copies):
        for copy in copies:
            copy.start()

    def wait(copies):
        for copy in copies:
            copy.wait()

    def at(condition, *steps):
        @pl.when(condition)
        def _():
            for step in steps:
                step()

    x_copy.start()
    g_copy.start()
    barrier = pltpu.get_barrier_semaphore()
    place.signal(barrier)
    place.wait(barrier)
    w0.send()
    x_copy.wait()

    def start_n0(k):
        def norm(h, rows):
            n0e[k, z, h, rows] = rms(xs[k, h, rows].astype(F32))
        by_rows(norm)
        rows_n0(k).start()
    loop(CHUNKS, start_n0)
    w0.step1()
    rows_n0(0).relay()
    w0.step2()
    loop(CHUNKS, lambda k: rows_n0(k).relay(), 1)
    w0.step3()
    w0.step4()
    loop(CHUNKS, lambda k: rows_n0(k).finish())
    n_save.start()
    g_copy.wait()
    w0.step5()
    w0.step6()
    loop(CHUNKS, lambda k: rows_g(k).start())
    w0.done()
    place.signal(phase.at[0])

    def close_o(k):
        rows_o(k).finish()

        def step(h, rows):
            o = rows_o.total(k, h, rows).astype(BF16).astype(F32)
            out = (xs[k, h, rows].astype(F32) + o).astype(BF16)
            hs[k, h, rows] = out
            n1[k, y, h, rows] = rms(out.astype(F32))
        by_rows(step)
        rows_n1(k).start()

    def forward(i):
        at(i >= 2, lambda: wait(saves(i - 2)))
        pre_acts(n0e, i, w0g, w0i, a_s, b_s, i % 2)
        at(i == 0, lambda: place.wait(phase.at[0]), w1.send)
        at(i == 1, w1.step2)
        at(i == 2, w1.step4)
        at(i == 3, w1.step5, rows_n1(0).relay)
        hidden(a_s, b_s, i % 2, u_s, i)
        start(saves(i))
        project(u_s, i, w0o, part)
        rows_o(i).start()
        at(i >= 1, lambda: rows_o(i - 1).relay())
        at(i == 0, w1.step1, lambda: loop(CHUNKS, lambda k: rows_g(k).relay()))
        at(i == 1, w1.step3)
        at(i >= 2, lambda: close_o(i - 2))
        at(i == 3, w1.step6)
    loop(CHUNKS, forward)
    rows_o(3).relay()
    wait(saves(2))
    wait(saves(3))
    n_save.wait()
    loop(CHUNKS, lambda k: rows_g(k).finish())
    w1.done()
    place.signal(phase.at[1])

    def close_1(k):
        rows_d1(k).finish()

        def step(h, rows):
            dn = rows_d1.total(k, h, rows)
            n0e[k, z, h, rows] = cotangent(hs[k, h, rows].astype(F32), ga[k, y, h, rows].astype(F32), dn)
        by_rows(step)
        rows_e(k).start()

    def middle(j):
        rows_n1(j).finish()
        pre_acts(n1, j, w1g, w1i, a_s, b_s, j % 2)
        hidden(a_s, b_s, j % 2, u_s, j)
        at(j <= 2, lambda: rows_n1(j + 1).relay())
        at(j <= 1, lambda: close_o(j + 2))
        at(j >= 1, lambda: rows_d1(j - 1).relay())
        at(j == 1, lambda: place.wait(phase.at[1]), w0b.send)
        at(j == 2, w0b.step1)
        at(j == 3, w0b.step3, rows_e(0).relay)
        hidden_back(ga, j, w1o, part, a_s, b_s, j % 2, da_s, db_s)
        input_back(da_s, db_s, j, w1g, w1i, part)
        rows_d1(j).start()
        at(j == 2, w0b.step2)
        at(j == 3, w0b.step4)
        at(j >= 2, lambda: start(loads(j - 2)), lambda: close_1(j - 2))
    loop(CHUNKS, middle)
    rows_d1(3).relay()
    weight_grad(u_s, ga, d_a)
    out1.swap()
    u_load.start()
    rows_e(1).relay()
    w0b.step5()
    weight_grad(n1, da_s, d_b)
    gate1.swap()
    close_1(2)
    w0b.step6()
    out1.combine()
    weight_grad(n1, db_s, d_a)
    inn1.swap()
    n_load.start()
    close_1(3)
    rows_e(2).relay()
    out1.first.relay()
    gate1.combine()
    w0b.done()

    def close_0(k):
        rows_d0(k).finish()

        def step(h, rows):
            dn = rows_d0.total(k, h, rows)
            dxs[k, h, rows] = cotangent(xs[k, h, rows].astype(F32), n0e[k, z, h, rows].astype(F32), dn)
        by_rows(step)

    def backward(i):
        rows_e(i).finish()
        wait(loads(i))
        hidden_back(n0e, i, w0o, part, a_s, b_s, i % 2, da_s, db_s)
        at(i <= 1, lambda: start(loads(i + 2)))
        at(i == 0, rows_e(3).relay, inn1.combine, gate1.first.relay)
        at(i == 1, inn1.first.relay, gate1.turn, out1.second.relay)
        at(i == 2, inn1.second.relay, gate1.last)
        at(i == 3, out1.done, gate1.done, inn1.done, lambda: place.signal(phase.at[2]))
        input_back(da_s, db_s, i, w0g, w0i, part)
        rows_d0(i).start()
        at(i >= 1, lambda: rows_d0(i - 1).relay())
        at(i == 0, out1.turn)
        at(i == 1, inn1.turn, gate1.second.relay, out1.last)
        at(i == 2, inn1.last)
        at(i >= 2, lambda: close_0(i - 2))
    loop(CHUNKS, backward)
    u_load.wait()
    weight_grad(u_s, n0e, d_a)
    place.wait(phase.at[2])
    out0.swap()
    rows_d0(3).relay()
    n_load.wait()
    weight_grad(n1, da_s, d_b)
    gate0.swap()
    close_0(2)
    out0.combine()
    weight_grad(n1, db_s, d_a)
    inn0.swap()
    out0.first.relay()
    gate0.combine()
    close_0(3)
    dx_slot, dx_local = place.slots(1), place.local_slots(1)
    dx_away, dx_here = place.remote(dxs, dx_out.at[c], place.partner, dx_slot), place.local(dxs, dx_out.at[c], dx_local)
    dx_away.start()
    dx_here.start()
    inn0.combine()
    gate0.first.relay()
    out0.turn()
    inn0.first.relay()
    out0.second.relay()
    gate0.turn()
    out0.last()
    inn0.turn()
    gate0.second.relay()
    gate0.last()
    inn0.second.relay()
    inn0.last()
    dx_away.wait()
    dx_here.wait()
    out0.done()
    gate0.done()
    inn0.done()


VM = pl.BlockSpec(memory_space=pltpu.VMEM)
ANY = pl.BlockSpec(memory_space=pl.ANY)


def sds(shape, dtype):
    return jax.ShapeDtypeStruct(shape, dtype)


ALL_ROWS = (CHUNKS, 4, 2, HALF, WIDE)
OWN_ROWS = (CHUNKS, 2, HALF, WIDE)
FLAT_ROWS = (CHUNKS, ROWS, WIDE)
WEIGHT = (4, 4, 4, 16, WIDE)
OUTS = [
    sds((2,) + OWN_ROWS, BF16), sds((16, 4 * WIDE), F32), sds((16, 4 * WIDE), F32), sds((4, 16, WIDE), F32),
    sds(FLAT_ROWS, F32), sds(FLAT_ROWS, F32), sds(FLAT_ROWS, BF16), sds(ALL_ROWS, BF16),
]
SCRATCH = (
    [pltpu.VMEM(OWN_ROWS, BF16)] * 3
    + [pltpu.VMEM(ALL_ROWS, BF16)] * 3
    + [pltpu.VMEM(FLAT_ROWS, BF16)]
    + [pltpu.VMEM((2, ROWS, WIDE), F32)] * 2
    + [pltpu.VMEM(FLAT_ROWS, BF16)] * 2
    + [pltpu.VMEM(ALL_ROWS, F32), pltpu.VMEM((3,) + OWN_ROWS, F32)]
    + [pltpu.VMEM(WEIGHT, BF16)] * 6
    + [pltpu.VMEM((4, 4, 2, 3, 16, WIDE), BF16)]
    + [pltpu.VMEM(WEIGHT, F32)] * 2
    + [
        pltpu.VMEM((3, 4, 4, 2, 16, WIDE), F32),
        pltpu.VMEM((3, 3, 2, 2, 2, 16, WIDE), F32),
        pltpu.VMEM((3, 4, 2, 16, WIDE), F32),
        pltpu.VMEM((3, 3, 2, 16, WIDE), F32),
        pltpu.VMEM((3, 2, 16, WIDE), F32),
    ]
    + [pltpu.SemaphoreType.DMA((N_REMOTE,)), pltpu.SemaphoreType.DMA((N_REMOTE,)), pltpu.SemaphoreType.DMA((N_LOCAL,))]
    + [pltpu.SemaphoreType.REGULAR((3,))]
)


def call(*operands):
    return pl.pallas_call(
        kernel,
        out_shape=OUTS,
        in_specs=[ANY] * 2 + [VM] * 3,
        out_specs=[ANY] * len(OUTS),
        scratch_shapes=SCRATCH,
        compiler_params=pltpu.CompilerParams(collective_id=1, has_side_effects=True, vmem_limit_bytes=67043328),
        name='kernel_all',
    )(*operands)


def solution(mesh):
    act_spec = P(None, 'data', None, None)
    weight_spec = P('stage', None, 'data', None)

    def per_device(x, g, w_gate, w_in, w_out):
        shards = (w_gate.reshape(16, 4 * WIDE), w_in.reshape(16, 4 * WIDE), w_out.reshape(4, 16, WIDE))
        dx, d_gate, d_in, d_out, *_ = call(x.reshape((2,) + OWN_ROWS), g.reshape((2,) + OWN_ROWS), *shards)
        return dx.reshape(x.shape), d_gate.reshape(w_gate.shape), d_in.reshape(w_in.shape), d_out.reshape(w_out.shape)

    return jax.shard_map(per_device, mesh=mesh, in_specs=(act_spec, act_spec, weight_spec, weight_spec, weight_spec), out_specs=(act_spec, weight_spec, weight_spec, weight_spec), check_vma=False)
```

time: 2510 us -> 291 us (0.12)
  waiting for transfers between devices: 1770 us -> 0 us
  matrix products: 583 us -> 0 us
  Pallas kernels: 0 us -> 282 us
  starting transfers between devices: 46 us -> 0 us
  other arithmetic: 43.2 us -> 0 us
  local copies, waits for them, and re-layouts: 44 us -> 7.3 us
    reduce_scatter x3 -> x0, waiting for transfers between devices: 1170 us -> none  [the longest x1 394 us: per_device(): lax.psum_scatter(jnp.stack(grad_sums[2]), 'data', scatter_dimension=1, ti...]
    dot_general x80 -> x0, matrix products: 583 us -> none  [the longest x8 161 us: layer_bwd(): jnp.einsum('td,tf->df', normed, d_gate, preferred_element_type=jnp.float32)]
    all_gather x6 -> x0, waiting for transfers between devices: 480 us -> none  [the longest x1 82 us: per_device(): gate_full = lax.all_gather(w_gate[0], 'data', axis=1, tiled=True)]
    pallas_call x0 -> x1, Pallas kernels: none -> 282 us  [call(): pl.pallas_call(kernel, out_shape=OUTS, in_specs=[ANY] * 2 + [VM] * 3, out...]
    ppermute x18 -> x0, waiting for transfers between devices: 86.8 us -> none  [the longest x9 78.2 us: bwd_tick(): sent_out = lax.ppermute(d_in, 'stage', bwd_pairs)]
    ppermute x18 -> x0, starting transfers between devices: 45.6 us -> none  [the longest x9 34 us: fwd_tick(): sent_out = lax.ppermute(block_out, 'stage', fwd_pairs)]
  transfers between devices with their start and end apart: 28 -> 0, of which waited for: 28 -> 0; matrix products, arithmetic and copies ran while one was open for 0% -> 0% of each run, Pallas kernels for 0% -> 0%
where the time goes in v3:
time: 291 us; the launch traced here: 290 us
  Pallas kernels  282 us (97%)
  local copies, waits for them, and re-layouts  7.3 us (3%)
    pallas_call x1, Pallas kernels, call(): pl.pallas_call(kernel, out_shape=OUTS, in_specs=[ANY] * 2 + [VM] * 3, out...  282 us
    unnamed x4, local copies, waits for them, and re-layouts  7.3 us

profile of v3, /device:TPU:0, one launch (start us, length us, event | category | flops | bytes accessed | tf_op | source)
XLA Modules:
  0.0 290.4 jit_solution(5501426886650004905)
XLA Ops:
  0.6 282.4 %kernel_all.1 = (bf16[2,4,2,32,1024]{4,3,2,1,0:T(8,128)(2,1)}, f32[16,4096]{1,0:T(8,128)}, f32[16,4096]{1,0:T(8,128)}, f32[4,16,1024]{2,1,0:T(8,128)}, f32[4,256...) custom-call(bf16[2,4,2,32,1024]{4,3,2,1,0:T(8,128)(2,1)} %bitcast.9,, ...), custom_call_target="tpu_custom_call" | custom-call | tf_op jit(solution)/shard_map/kernel_all/pallas_call | solution.py:804
  283.1 2.3 copy.13
  285.4 1.7 copy.14
  287.0 1.7 copy.15
  288.7 1.7 copy.16

commit v4 on v3

--- a/solution.py
+++ b/solution.py
@@ -15,9 +15,10 @@
 HALF = 128 // CHUNKS
 ROWS = 8 * HALF
 STEP = 16
+GROUPS = ROWS // STEP
 COLS = 512
 WIDE = 1024
-N_REMOTE = 224
+N_REMOTE = 280
 N_LOCAL = 40
 
 
@@ -68,21 +69,31 @@
 
 
 class Block:
-    def __init__(self, place, b):
+    def __init__(self, place, b, heavy):
         self.b, self.c, self.x = b, place.c, place.x
         self.t, self.w = (place.z, place.y) if b == 0 else (place.y, place.z)
-        t, w, x, c, k = self.t, self.w, self.x, self.c, 1 - self.c
+        self.heavy = heavy
+        t, w, x, c = self.t, self.w, self.x, self.c
         self.a1, self.a2 = self.order(w, x, c)
         self.rows = (t, self.dev((t + 1) % 4, w, x, c), self.dev((t + 3) % 4, w, x, c))
-        self.ring1 = (self.a1, self.dev(t, (w + c) % 4, (x + k) % 4, c), self.dev(t, (w + 3 * c) % 4, (x + 3 * k) % 4, c))
-        self.ring2 = (self.a2, self.dev(t, (w + k) % 4, (x + c) % 4, c), self.dev(t, (w + 3 * k) % 4, (x + 3 * c) % 4, c))
+        v = self.turned(c)
+        k = 1 - v
+        self.ring1 = (self.a1, self.dev(t, (w + v) % 4, (x + k) % 4, c), self.dev(t, (w + 3 * v) % 4, (x + 3 * k) % 4, c))
+        self.ring2 = (self.a2, self.dev(t, (w + k) % 4, (x + v) % 4, c), self.dev(t, (w + 3 * k) % 4, (x + 3 * v) % 4, c))
 
     def dev(self, t, w, x, c):
         return Place.dev(t, w, x, c) if self.b == 0 else Place.dev(w, t, x, c)
 
-    @staticmethod
-    def order(w, x, c):
-        return (1 - c) * x + c * w, (1 - c) * w + c * x
+    def turned(self, core):
+        return core if self.heavy == 'split' else int(self.heavy == 'w')
+
+    def order(self, w, x, core):
+        v = self.turned(core)
+        return (1 - v) * x + v * w, (1 - v) * w + v * x
+
+    def place(self, a1, a2, core):
+        v = self.turned(core)
+        return (1 - v) * a2 + v * a1, (1 - v) * a1 + v * a2
 
     def index(self, m, w, x, q):
         return (w, x, q) if m == 2 else (q, w, x) if self.b == 0 else (w, q, x)
@@ -231,8 +242,11 @@
         self.pl, self.bk, self.s, self.shards, self.held, self.outs = place, block, block.b, shards, held, outs
         self.slots, self.out_slot, self.swap_slots = base, base + 8, base + 9
         self.local, self.copy_local = local, local + 3
-        self.first = Gather(place, block.ring2, lambda j, h: held.at[block.a1, j, h], base + 12)
-        self.second = Gather(place, block.ring1, lambda j, h: held.at[j, 2 * h:2 * h + 2], base + 18)
+        self.first = Gather(place, block.ring2, lambda j, h: held.at[block.a1, pl.ds((2 * j + h) * 3, 3)], base + 12)
+        self.second = Gather(place, block.ring1, lambda j, h: held.at[j, 12 * h:12 * h + 12], base + 18)
+
+    def piece(self, a1, a2, q, m):
+        return self.held.at[a1, (2 * a2 + q) * 3 + m]
 
     def parts(self, dz):
         bk = self.bk
@@ -240,13 +254,14 @@
         core = bk.t // 2
         a1, a2 = bk.order(bk.w, bk.x, core)
         for m in range(2):
-            whole = self.held.at[a1, a2, bk.t % 2, m]
-            copies = [(self.shards[m].at[:, src], self.held.at[a1, a2, bk.t % 2, m, :, dst]) for src, dst in bk.pieces(target)]
+            whole = self.piece(a1, a2, bk.t % 2, m)
+            copies = [(self.shards[m].at[:, src], whole.at[:, dst]) for src, dst in bk.pieces(target)]
             yield m, copies, whole, bk.dev(target, bk.w, bk.x, core)
 
     def out_part(self, core):
         a1, a2 = self.bk.order(self.bk.w, self.bk.x, core)
-        return self.shards[2].at[2 * core:2 * core + 2], self.held.at[a1, a2, :, 2]
+        copies = [(self.shards[2].at[2 * core + q], self.piece(a1, a2, q, 2)) for q in range(2)]
+        return copies, self.held.at[a1, pl.ds(0, 2)]
 
     def source(self, wait):
         place, s = self.pl, self.s
@@ -281,10 +296,8 @@
             def _():
                 for m, copies, whole, _ in self.parts(0):
                     away(copies, whole, place.partner, self.slots + m)
-            src, dst = self.out_part(s)
-            here([(src, dst)], dst, self.local + 2)
-            src, dst = self.out_part(1 - s)
-            away([(src, dst)], dst, place.partner, self.out_slot)
+            here(*self.out_part(s), self.local + 2)
+            away(*self.out_part(1 - s), place.partner, self.out_slot)
 
     def send(self):
         self.source(False)
@@ -300,26 +313,27 @@
             @pl.when(here)
             def _(dz=dz, source=source):
                 for m in range(2):
-                    dst = self.held.at[bk.a1, bk.a2, source % 2, m]
+                    dst = self.piece(bk.a1, bk.a2, source % 2, m)
                     place.remote(dst, dst, place.partner, self.slots + 2 * dz + m).wait_recv()
 
         self.source(True)
 
         @pl.when(place.c != s)
         def _():
-            _, dst = self.out_part(1 - s)
-            place.remote(dst, dst, place.partner, self.out_slot).wait_recv()
+            _, whole = self.out_part(1 - s)
+            place.remote(whole, whole, place.partner, self.out_slot).wait_recv()
 
     def spread(self, a1):
         place, bk = self.pl, self.bk
 
         def one(a2):
-            x, w = bk.order(a2, a1, place.c)
+            w, x = bk.place(a1, a2, place.c)
             for m in range(3):
-                src = self.held.at[a1, a2, :, m]
-                dst = self.outs[m].at[bk.index(m, w, x, pair(place.c))]
-                place.remote(src, dst, place.partner, self.swap_slots + m).start()
-                place.local(src, dst, self.copy_local + m).start()
+                for q in range(2):
+                    src = self.piece(a1, a2, q, m)
+                    dst = self.outs[m].at[bk.index(m, w, x, 2 * place.c + q)]
+                    place.remote(src, dst, place.partner, self.swap_slots + m).start()
+                    place.local(src, dst, self.copy_local + m).start()
         loop(4, one)
 
     def done(self):
@@ -357,11 +371,11 @@
 
 
 class Grads:
-    def __init__(self, place, block, m, part, bufs, out, base, local):
+    def __init__(self, place, block, m, part, bufs, kit, out, base, local):
         self.pl, self.bk, self.s, self.m, self.part, self.out = place, block, block.b, m, part, out
-        mine, held1, sum1, held2, sum2 = (buf.at[m] for buf in bufs)
-        self.mine, self.held1, self.sum1, self.held2, self.sum2 = mine, held1, sum1, held2, sum2
-        base, self.local = base + 17 * m, local + m
+        mine, held1, held2, sum2 = (buf.at[kit] for buf in bufs)
+        self.mine, self.held1, self.held2, self.sum2 = mine, held1, held2, sum2
+        self.local = local
         self.swap_slot, self.hand_slots = base, base + 1
 
         def add1(h, j):
@@ -372,8 +386,8 @@
         self.first = Reduce(place, block.ring1, lambda j, h: mine.at[j, 2 * h:2 * h + 2], lambda b: held1.at[b], add1, base + 5)
 
         def add2(h, j):
-            held2[0, h] = held2[0, h] + sum1[j, h]
-        self.second = Reduce(place, block.ring2, lambda j, h: sum1.at[j, h], lambda b: held2.at[b], add2, base + 11)
+            held2[0, h] = held2[0, h] + mine[block.a1, j, h]
+        self.second = Reduce(place, block.ring2, lambda j, h: mine.at[block.a1, j, h], lambda b: held2.at[b], add2, base + 11)
 
     def swap(self):
         place, bk = self.pl, self.bk
@@ -396,23 +410,22 @@
             for q in range(2):
                 mine[a1, a2, q] = mine[a1, a2, q] + self.part[bk.index(self.m, w, x, 2 * place.c + q)]
         loop(16, one)
-        self.first.start()
         whole.wait_send()
 
     def turn(self):
-        bk, mine, held1, sum1 = self.bk, self.mine, self.held1, self.sum1
+        bk, mine, held1 = self.bk, self.mine, self.held1
         self.first.finish()
 
         def one(i):
             h, k, q = i // 4, i // 2 % 2, i % 2
-            sum1[i // 2, q] = mine[bk.a1, i // 2, q] + held1[1, h, k, q] + held1[2, h, k, q]
+            mine[bk.a1, i // 2, q] = mine[bk.a1, i // 2, q] + held1[1, h, k, q] + held1[2, h, k, q]
         loop(8, one)
         self.second.start()
 
     def last(self):
         self.second.finish()
         for h in range(2):
-            self.sum2[h] = self.sum1[self.bk.a2, h] + self.held2[1, h] + self.held2[2, h]
+            self.sum2[h] = self.mine[self.bk.a1, self.bk.a2, h] + self.held2[1, h] + self.held2[2, h]
         self.hand(False)
 
     def hand(self, wait):
@@ -504,7 +517,7 @@
     part[k] = mm(u_ref[k], square(out)).reshape(4, 2, HALF, WIDE)
 
 
-def hidden_back(e_ref, k, out, t_ref, a_ref, b_ref, slot, da_ref, db_ref):
+def hidden_back(e_ref, k, out, t_ref, a_ref, b_ref, slot, dab):
     t_ref[k] = mm_nt(chunk(e_ref, k), square(out)).reshape(4, 2, HALF, WIDE)
     per_half = HALF // STEP
 
@@ -515,15 +528,16 @@
         t = t_ref[k, j, h, pl.ds(pl.multiple_of(i % per_half * STEP, STEP), STEP)]
         a, b = a_ref[slot, rows], b_ref[slot, rows]
         s = jax.nn.sigmoid(a)
-        da_ref[k, rows] = (t * b * s * (1.0 + a * (1.0 - s))).astype(BF16)
-        db_ref[k, rows] = (t * a * s).astype(BF16)
+        dab[k, i] = (t * b * s * (1.0 + a * (1.0 - s))).astype(BF16)
+        dab[k, GROUPS + i] = (t * a * s).astype(BF16)
     loop(ROWS // STEP, one)
 
 
-def input_back(da_ref, db_ref, k, gate, inn, part):
+def input_back(dab, k, gate, inn, part):
     def one(i):
+        da, db = dab[k, :GROUPS].reshape(ROWS, WIDE), dab[k, GROUPS:].reshape(ROWS, WIDE)
         cols = pl.ds(pl.multiple_of(i * COLS, COLS), COLS)
-        dn = mm_nt(da_ref[k], gate[pl.ds(2 * i, 2)].reshape(COLS, WIDE)) + mm_nt(db_ref[k], inn[pl.ds(2 * i, 2)].reshape(COLS, WIDE))
+        dn = mm_nt(da, gate[pl.ds(2 * i, 2)].reshape(COLS, WIDE)) + mm_nt(db, inn[pl.ds(2 * i, 2)].reshape(COLS, WIDE))
         part[k, :, :, :, cols] = dn.reshape(4, 2, HALF, COLS)
     loop(WIDE // COLS, one)
 
@@ -536,28 +550,41 @@
     loop(4, one)
 
 
-def kernel(x_in, g_in, wg, wi, wo, dx_out, gg, gi, go, a_out, b_out, u_out, n_out,
-           xs, hs, dxs, n0e, n1, ga, u_s, a_s, b_s, da_s, db_s, part, held, w0g, w0i, w0o, w1g, w1i, w1o, held_w,
-           d_a, d_b, mine, held1, sum1, held2, sum2, ssem, rsem, lsem, phase):
+def weight_grad_of(n_ref, dab, first, out):
+    def one(i):
+        cols = pl.ds(pl.multiple_of(i * 256, 256), 256)
+        right = dab[:, first:first + GROUPS].reshape(CHUNKS * ROWS, WIDE)
+        out[i] = mm_tn(n_ref[..., cols].reshape(CHUNKS * ROWS, 256), right).reshape(4, 4, 16, WIDE)
+    loop(4, one)
+
+
+HEAVY = {'w0': 'split', 'w1': 'x', 'v0': 'x', 'out1': 'x', 'gate1': 'split', 'inn1': 'split', 'out0': 'split', 'gate0': 'split', 'inn0': 'split'}
+
+
+def kernel(x_in, g_in, wg, wi, wo, dx_out, gg, gi, go, a_out, b_out, u_out, n_out, held_1, held_0,
+           xs, hs, n0e, n1, ga, u_s, a_s, b_s, dab, part, held, w0g, w0i, w0o, w1g, w1i, w1o,
+           d_a, d_b, mine, held1, held2, sum2, ssem, rsem, lsem, phase):
     place = Place(ssem, rsem, lsem, phase)
     z, y, c = place.z, place.y, place.c
-    blocks = Block(place, 0), Block(place, 1)
+    rows0, rows1 = Block(place, 0, 'x').rows, Block(place, 1, 'x').rows
     per_row = 6 * CHUNKS
     z_gather, z_sum, g_gather, y_gather, y_sum = (place.slots(per_row) for _ in range(5))
-    rows_n0, rows_e = (Spreads(place, blocks[0].rows, n0e, z_gather) for _ in range(2))
-    rows_o, rows_d0 = (Rows(place, blocks[0].rows, part, held, z_sum) for _ in range(2))
-    rows_g = Spreads(place, blocks[1].rows, ga, g_gather)
-    rows_n1 = Spreads(place, blocks[1].rows, n1, y_gather)
-    rows_d1 = Rows(place, blocks[1].rows, part, held, y_sum)
+    n0, e = (Spreads(place, rows0, n0e, z_gather) for _ in range(2))
+    o, d0 = (Rows(place, rows0, part, held, z_sum) for _ in range(2))
+    g = Spreads(place, rows1, ga, g_gather)
+    n = Spreads(place, rows1, n1, y_gather)
+    d1 = Rows(place, rows1, part, held, y_sum)
     shards = (wg, wi, wo)
     w0_slots, w0_local = place.slots(24), place.local_slots(6)
-    w0, w0b = (Weights(place, blocks[0], shards, held_w, (w0g, w0i, w0o), w0_slots, w0_local) for _ in range(2))
-    w1 = Weights(place, blocks[1], shards, held_w, (w1g, w1i, w1o), place.slots(24), place.local_slots(6))
-    grad_slots, grad_local = place.slots(51), place.local_slots(3)
-    bufs, outs = (mine, held1, sum1, held2, sum2), (gg, gi, go)
-    (gate1, inn1, out1), (gate0, inn0, out0) = (
-        [Grads(place, blocks[b], m, (d_b, d_a, d_a)[m], bufs, outs[m], grad_slots, grad_local) for m in range(3)] for b in (1, 0)
-    )
+    w0 = Weights(place, Block(place, 0, HEAVY['w0']), shards, dab, (w0g, w0i, w0o), w0_slots, w0_local)
+    v0 = Weights(place, Block(place, 0, HEAVY['v0']), shards, held_0, (w0g, w0i, w0o), w0_slots, w0_local)
+    w1 = Weights(place, Block(place, 1, HEAVY['w1']), shards, held_1, (w1g, w1i, w1o), place.slots(24), place.local_slots(6))
+    bufs, outs = (mine, held1, held2, sum2), (gg, gi, go)
+
+    def grads(b, m, part, kit, heavy):
+        return Grads(place, Block(place, b, heavy), m, part, bufs, kit, outs[m], place.slots(17), place.local_slots(1))
+    out1, gate1, inn1 = grads(1, 2, d_a, 0, HEAVY['out1']), grads(1, 0, d_b, 1, HEAVY['gate1']), grads(1, 1, d_a, 2, HEAVY['inn1'])
+    out0, gate0, inn0 = grads(0, 2, d_b, 3, HEAVY['out0']), grads(0, 0, d_a, 0, HEAVY['gate0']), grads(0, 1, d_b, 1, HEAVY['inn0'])
     x_copy = place.local(x_in.at[c], xs, place.local_slots(1))
     g_copy = place.local(g_in.at[c], ga.at[:, y], place.local_slots(1))
     save = place.local_slots(8)
@@ -582,11 +609,59 @@
         for copy in copies:
             copy.wait()
 
-    def at(condition, *steps):
-        @pl.when(condition)
-        def _():
-            for step in steps:
-                step()
+    def forward(k):
+        if k >= 2:
+            wait(saves(k - 2))
+        pre_acts(n0e, k, w0g, w0i, a_s, b_s, k % 2)
+        hidden(a_s, b_s, k % 2, u_s, k)
+        start(saves(k))
+        project(u_s, k, w0o, part)
+
+    def close_o(k):
+        o(k).finish()
+
+        def step(h, rows):
+            total = o.total(k, h, rows).astype(BF16).astype(F32)
+            out = (xs[k, h, rows].astype(F32) + total).astype(BF16)
+            hs[k, h, rows] = out
+            n1[k, y, h, rows] = rms(out.astype(F32))
+        by_rows(step)
+        n(k).start()
+
+    def middle(k):
+        n(k).finish()
+        pre_acts(n1, k, w1g, w1i, a_s, b_s, k % 2)
+        hidden(a_s, b_s, k % 2, u_s, k)
+        hidden_back(ga, k, w1o, part, a_s, b_s, k % 2, dab)
+        input_back(dab, k, w1g, w1i, part)
+
+    def close_1(k):
+        d1(k).finish()
+
+        def step(h, rows):
+            dn = d1.total(k, h, rows)
+            n0e[k, z, h, rows] = cotangent(hs[k, h, rows].astype(F32), ga[k, y, h, rows].astype(F32), dn)
+        by_rows(step)
+        e(k).start()
+
+    def back_hidden(k):
+        e(k).finish()
+        wait(loads(k))
+        hidden_back(n0e, k, w0o, part, a_s, b_s, k % 2, dab)
+        if k < 2:
+            start(loads(k + 2))
+
+    def back_input(k):
+        input_back(dab, k, w0g, w0i, part)
+        d0(k).start()
+
+    def close_0(k):
+        d0(k).finish()
+
+        def step(h, rows):
+            dn = d0.total(k, h, rows)
+            hs[k, h, rows] = cotangent(xs[k, h, rows].astype(F32), n0e[k, z, h, rows].astype(F32), dn)
+        by_rows(step)
 
     x_copy.start()
     g_copy.start()
@@ -594,165 +669,179 @@
     place.signal(barrier)
     place.wait(barrier)
     w0.send()
+    w1.send()
     x_copy.wait()
 
     def start_n0(k):
         def norm(h, rows):
             n0e[k, z, h, rows] = rms(xs[k, h, rows].astype(F32))
         by_rows(norm)
-        rows_n0(k).start()
+        n0(k).start()
     loop(CHUNKS, start_n0)
     w0.step1()
-    rows_n0(0).relay()
+    n0(0).relay()
     w0.step2()
-    loop(CHUNKS, lambda k: rows_n0(k).relay(), 1)
+    n0(1).relay()
     w0.step3()
+    n0(2).relay()
+    n0(3).relay()
+    w1.step1()
     w0.step4()
-    loop(CHUNKS, lambda k: rows_n0(k).finish())
+    loop(CHUNKS, lambda k: n0(k).finish())
     n_save.start()
+    w1.step2()
+    w0.step5()
     g_copy.wait()
-    w0.step5()
+    loop(CHUNKS, lambda k: g(k).start())
+    w1.step3()
     w0.step6()
-    loop(CHUNKS, lambda k: rows_g(k).start())
     w0.done()
+
+    forward(0)
+    o(0).start()
+    forward(1)
+    g(0).relay()
+    g(1).relay()
+    o(0).relay()
+    o(1).start()
+    forward(2)
+    g(2).relay()
+    w1.step4()
+    g(3).relay()
+    close_o(0)
+    o(1).relay()
+    o(2).start()
+    forward(3)
+    n_save.wait()
     place.signal(phase.at[0])
-
-    def close_o(k):
-        rows_o(k).finish()
-
-        def step(h, rows):
-            o = rows_o.total(k, h, rows).astype(BF16).astype(F32)
-            out = (xs[k, h, rows].astype(F32) + o).astype(BF16)
-            hs[k, h, rows] = out
-            n1[k, y, h, rows] = rms(out.astype(F32))
-        by_rows(step)
-        rows_n1(k).start()
-
-    def forward(i):
-        at(i >= 2, lambda: wait(saves(i - 2)))
-        pre_acts(n0e, i, w0g, w0i, a_s, b_s, i % 2)
-        at(i == 0, lambda: place.wait(phase.at[0]), w1.send)
-        at(i == 1, w1.step2)
-        at(i == 2, w1.step4)
-        at(i == 3, w1.step5, rows_n1(0).relay)
-        hidden(a_s, b_s, i % 2, u_s, i)
-        start(saves(i))
-        project(u_s, i, w0o, part)
-        rows_o(i).start()
-        at(i >= 1, lambda: rows_o(i - 1).relay())
-        at(i == 0, w1.step1, lambda: loop(CHUNKS, lambda k: rows_g(k).relay()))
-        at(i == 1, w1.step3)
-        at(i >= 2, lambda: close_o(i - 2))
-        at(i == 3, w1.step6)
-    loop(CHUNKS, forward)
-    rows_o(3).relay()
+    v0.send()
+    n(0).relay()
+    w1.step5()
+    o(2).relay()
+    o(3).start()
+    loop(CHUNKS, lambda k: g(k).finish())
     wait(saves(2))
     wait(saves(3))
-    n_save.wait()
-    loop(CHUNKS, lambda k: rows_g(k).finish())
+    w1.step6()
+    close_o(1)
     w1.done()
-    place.signal(phase.at[1])
-
-    def close_1(k):
-        rows_d1(k).finish()
-
-        def step(h, rows):
-            dn = rows_d1.total(k, h, rows)
-            n0e[k, z, h, rows] = cotangent(hs[k, h, rows].astype(F32), ga[k, y, h, rows].astype(F32), dn)
-        by_rows(step)
-        rows_e(k).start()
-
-    def middle(j):
-        rows_n1(j).finish()
-        pre_acts(n1, j, w1g, w1i, a_s, b_s, j % 2)
-        hidden(a_s, b_s, j % 2, u_s, j)
-        at(j <= 2, lambda: rows_n1(j + 1).relay())
-        at(j <= 1, lambda: close_o(j + 2))
-        at(j >= 1, lambda: rows_d1(j - 1).relay())
-        at(j == 1, lambda: place.wait(phase.at[1]), w0b.send)
-        at(j == 2, w0b.step1)
-        at(j == 3, w0b.step3, rows_e(0).relay)
-        hidden_back(ga, j, w1o, part, a_s, b_s, j % 2, da_s, db_s)
-        input_back(da_s, db_s, j, w1g, w1i, part)
-        rows_d1(j).start()
-        at(j == 2, w0b.step2)
-        at(j == 3, w0b.step4)
-        at(j >= 2, lambda: start(loads(j - 2)), lambda: close_1(j - 2))
-    loop(CHUNKS, middle)
-    rows_d1(3).relay()
+
+    middle(0)
+    n(1).relay()
+    d1(0).start()
+    o(3).relay()
+    v0.step1()
+    close_o(2)
+    middle(1)
+    n(2).relay()
+    d1(0).relay()
+    d1(1).start()
+    v0.step2()
+    close_o(3)
+    middle(2)
+    n(3).relay()
+    d1(1).relay()
+    d1(2).start()
+    place.wait(phase.at[0])
+    v0.step3()
+    start(loads(0))
+    close_1(0)
+    middle(3)
+    d1(2).relay()
+    d1(3).start()
+    start(loads(1))
+    e(0).relay()
+    v0.step4()
     weight_grad(u_s, ga, d_a)
     out1.swap()
     u_load.start()
-    rows_e(1).relay()
-    w0b.step5()
-    weight_grad(n1, da_s, d_b)
+    close_1(1)
+    weight_grad_of(n1, dab, 0, d_b)
     gate1.swap()
-    close_1(2)
-    w0b.step6()
+    d1(3).relay()
+    v0.step5()
     out1.combine()
-    weight_grad(n1, db_s, d_a)
+    out1.first.start()
+    e(1).relay()
+    weight_grad_of(n1, dab, GROUPS, d_a)
     inn1.swap()
     n_load.start()
+    close_1(2)
+    gate1.combine()
+    v0.step6()
     close_1(3)
-    rows_e(2).relay()
+    v0.done()
+
+    e(2).relay()
+    back_hidden(0)
+    e(3).relay()
+    inn1.combine()
+    gate1.first.start()
+    back_hidden(1)
     out1.first.relay()
-    gate1.combine()
-    w0b.done()
-
-    def close_0(k):
-        rows_d0(k).finish()
-
-        def step(h, rows):
-            dn = rows_d0.total(k, h, rows)
-            dxs[k, h, rows] = cotangent(xs[k, h, rows].astype(F32), n0e[k, z, h, rows].astype(F32), dn)
-        by_rows(step)
-
-    def backward(i):
-        rows_e(i).finish()
-        wait(loads(i))
-        hidden_back(n0e, i, w0o, part, a_s, b_s, i % 2, da_s, db_s)
-        at(i <= 1, lambda: start(loads(i + 2)))
-        at(i == 0, rows_e(3).relay, inn1.combine, gate1.first.relay)
-        at(i == 1, inn1.first.relay, gate1.turn, out1.second.relay)
-        at(i == 2, inn1.second.relay, gate1.last)
-        at(i == 3, out1.done, gate1.done, inn1.done, lambda: place.signal(phase.at[2]))
-        input_back(da_s, db_s, i, w0g, w0i, part)
-        rows_d0(i).start()
-        at(i >= 1, lambda: rows_d0(i - 1).relay())
-        at(i == 0, out1.turn)
-        at(i == 1, inn1.turn, gate1.second.relay, out1.last)
-        at(i == 2, inn1.last)
-        at(i >= 2, lambda: close_0(i - 2))
-    loop(CHUNKS, backward)
+    back_hidden(2)
     u_load.wait()
-    weight_grad(u_s, n0e, d_a)
+    n_load.wait()
+    inn1.first.start()
+    e(3).finish()
+    weight_grad(u_s, n0e, d_b)
+    out0.swap()
+    gate1.first.relay()
+    wait(loads(3))
+    hidden_back(n0e, 3, w0o, part, a_s, b_s, 1, dab)
+    out1.turn()
+    weight_grad_of(n1, dab, 0, d_a)
+    out0.combine()
+    out0.first.start()
+    back_input(0)
+    inn1.first.relay()
+    weight_grad_of(n1, dab, GROUPS, d_b)
+    out1.second.relay()
+    back_input(1)
+    d0(0).relay()
+    out0.first.relay()
+    out1.last()
+    gate1.turn()
+    back_input(2)
+    d0(1).relay()
+    out1.done()
+    place.signal(phase.at[1])
+    back_input(3)
+    gate1.second.relay()
+    d0(2).relay()
+    place.wait(phase.at[1])
+    gate0.swap()
+    inn1.turn()
+    gate0.combine()
+    gate0.first.start()
+    gate1.last()
+    out0.turn()
+    gate1.done()
+    place.signal(phase.at[2])
+    inn1.second.relay()
+    close_0(0)
+    d0(3).relay()
     place.wait(phase.at[2])
-    out0.swap()
-    rows_d0(3).relay()
-    n_load.wait()
-    weight_grad(n1, da_s, d_b)
-    gate0.swap()
+    inn0.swap()
+    gate0.first.relay()
+    out0.second.relay()
+    inn0.combine()
+    inn0.first.start()
+    inn1.last()
+    close_0(1)
+    gate0.turn()
+    inn0.first.relay()
     close_0(2)
-    out0.combine()
-    weight_grad(n1, db_s, d_a)
-    inn0.swap()
-    out0.first.relay()
-    gate0.combine()
+    out0.last()
     close_0(3)
     dx_slot, dx_local = place.slots(1), place.local_slots(1)
-    dx_away, dx_here = place.remote(dxs, dx_out.at[c], place.partner, dx_slot), place.local(dxs, dx_out.at[c], dx_local)
+    dx_away, dx_here = place.remote(hs, dx_out.at[c], place.partner, dx_slot), place.local(hs, dx_out.at[c], dx_local)
     dx_away.start()
     dx_here.start()
-    inn0.combine()
-    gate0.first.relay()
-    out0.turn()
-    inn0.first.relay()
-    out0.second.relay()
-    gate0.turn()
-    out0.last()
+    gate0.second.relay()
     inn0.turn()
-    gate0.second.relay()
     gate0.last()
+    inn1.done()
     inn0.second.relay()
     inn0.last()
     dx_away.wait()
@@ -774,26 +863,26 @@
 OWN_ROWS = (CHUNKS, 2, HALF, WIDE)
 FLAT_ROWS = (CHUNKS, ROWS, WIDE)
 WEIGHT = (4, 4, 4, 16, WIDE)
+STAGED = (4, 24, 16, WIDE)
 OUTS = [
     sds((2,) + OWN_ROWS, BF16), sds((16, 4 * WIDE), F32), sds((16, 4 * WIDE), F32), sds((4, 16, WIDE), F32),
     sds(FLAT_ROWS, F32), sds(FLAT_ROWS, F32), sds(FLAT_ROWS, BF16), sds(ALL_ROWS, BF16),
+    sds(STAGED, BF16), sds(STAGED, BF16),
 ]
 SCRATCH = (
-    [pltpu.VMEM(OWN_ROWS, BF16)] * 3
+    [pltpu.VMEM(OWN_ROWS, BF16)] * 2
     + [pltpu.VMEM(ALL_ROWS, BF16)] * 3
     + [pltpu.VMEM(FLAT_ROWS, BF16)]
     + [pltpu.VMEM((2, ROWS, WIDE), F32)] * 2
-    + [pltpu.VMEM(FLAT_ROWS, BF16)] * 2
+    + [pltpu.VMEM((CHUNKS, 2 * GROUPS, STEP, WIDE), BF16)]
     + [pltpu.VMEM(ALL_ROWS, F32), pltpu.VMEM((3,) + OWN_ROWS, F32)]
     + [pltpu.VMEM(WEIGHT, BF16)] * 6
-    + [pltpu.VMEM((4, 4, 2, 3, 16, WIDE), BF16)]
     + [pltpu.VMEM(WEIGHT, F32)] * 2
     + [
-        pltpu.VMEM((3, 4, 4, 2, 16, WIDE), F32),
-        pltpu.VMEM((3, 3, 2, 2, 2, 16, WIDE), F32),
-        pltpu.VMEM((3, 4, 2, 16, WIDE), F32),
-        pltpu.VMEM((3, 3, 2, 16, WIDE), F32),
-        pltpu.VMEM((3, 2, 16, WIDE), F32),
+        pltpu.VMEM((4, 4, 4, 2, 16, WIDE), F32),
+        pltpu.VMEM((4, 3, 2, 2, 2, 16, WIDE), F32),
+        pltpu.VMEM((4, 3, 2, 16, WIDE), F32),
+        pltpu.VMEM((4, 2, 16, WIDE), F32),
     ]
     + [pltpu.SemaphoreType.DMA((N_REMOTE,)), pltpu.SemaphoreType.DMA((N_REMOTE,)), pltpu.SemaphoreType.DMA((N_LOCAL,))]
     + [pltpu.SemaphoreType.REGULAR((3,))]

time: 291 us -> 241 us (0.83)
  Pallas kernels: 282 us -> 233 us
    pallas_call x1, Pallas kernels: 282 us -> 233 us  [call(): pl.pallas_call(kernel, out_shape=OUTS, in_specs=[ANY] * 2 + [VM] * 3, out...]
    unnamed x4 -> x6, local copies, waits for them, and re-layouts: 7.3 us -> 6.37 us
where the time goes in v4:
time: 241 us; the launch traced here: 240 us
  Pallas kernels  233 us (97%)
  local copies, waits for them, and re-layouts  6.37 us (3%)
    pallas_call x1, Pallas kernels, call(): pl.pallas_call(kernel, out_shape=OUTS, in_specs=[ANY] * 2 + [VM] * 3, out...  233 us
    unnamed x6, local copies, waits for them, and re-layouts  6.37 us

profile of v4, /device:TPU:0, one launch (start us, length us, event | category | flops | bytes accessed | tf_op | source)
XLA Modules:
  0.0 240.4 jit_solution(9174291123918582593)
XLA Ops:
  0.6 233.4 %kernel_all.1 = (bf16[2,4,2,32,1024]{4,3,2,1,0:T(8,128)(2,1)}, f32[16,4096]{1,0:T(8,128)}, f32[16,4096]{1,0:T(8,128)}, f32[4,16,1024]{2,1,0:T(8,128)}, f32[4,256...) custom-call(bf16[2,4,2,32,1024]{4,3,2,1,0:T(8,128)(2,1)} %bitcast.9,, ...), custom_call_target="tpu_custom_call" | custom-call | tf_op jit(solution)/shard_map/kernel_all/pallas_call | solution.py:893
  234.1 0.0 copy-start
  234.1 2.3 copy.13
  236.4 1.7 copy.14
  238.1 1.7 copy.15
  239.7 0.0 copy-done
  239.7 0.7 copy.16
Async XLA Ops:
  234.1 5.7 %copy-start = (f32[4,16,1024]{2,1,0:T(8,128)S(1)}, f32[4,16,1024]{2,1,0:T(8,128)}, u32[]{:S(2)}) copy-start(f32[4,16,1024]{2,1,0:T(8,128)} %get-tuple-element.11) | copy-start | bytes 786436

commit v5 on v4

--- a/solution.py
+++ b/solution.py
@@ -371,9 +371,9 @@
 
 
 class Grads:
-    def __init__(self, place, block, m, part, bufs, kit, out, base, local):
+    def __init__(self, place, block, m, part, kit, out, base, local):
         self.pl, self.bk, self.s, self.m, self.part, self.out = place, block, block.b, m, part, out
-        mine, held1, held2, sum2 = (buf.at[kit] for buf in bufs)
+        mine, held1, held2, sum2 = kit
         self.mine, self.held1, self.held2, self.sum2 = mine, held1, held2, sum2
         self.local = local
         self.swap_slot, self.hand_slots = base, base + 1
@@ -558,7 +558,7 @@
     loop(4, one)
 
 
-HEAVY = {'w0': 'split', 'w1': 'x', 'v0': 'x', 'out1': 'x', 'gate1': 'split', 'inn1': 'split', 'out0': 'split', 'gate0': 'split', 'inn0': 'split'}
+HEAVY = {'w0': 'split', 'w1': 'x', 'v0': 'x', 'out1': 'x', 'gate1': 'split', 'in1': 'split', 'out0': 'split', 'gate0': 'split', 'in0': 'split'}
 
 
 def kernel(x_in, g_in, wg, wi, wo, dx_out, gg, gi, go, a_out, b_out, u_out, n_out, held_1, held_0,
@@ -579,12 +579,14 @@
     w0 = Weights(place, Block(place, 0, HEAVY['w0']), shards, dab, (w0g, w0i, w0o), w0_slots, w0_local)
     v0 = Weights(place, Block(place, 0, HEAVY['v0']), shards, held_0, (w0g, w0i, w0o), w0_slots, w0_local)
     w1 = Weights(place, Block(place, 1, HEAVY['w1']), shards, held_1, (w1g, w1i, w1o), place.slots(24), place.local_slots(6))
-    bufs, outs = (mine, held1, held2, sum2), (gg, gi, go)
-
-    def grads(b, m, part, kit, heavy):
-        return Grads(place, Block(place, b, heavy), m, part, bufs, kit, outs[m], place.slots(17), place.local_slots(1))
-    out1, gate1, inn1 = grads(1, 2, d_a, 0, HEAVY['out1']), grads(1, 0, d_b, 1, HEAVY['gate1']), grads(1, 1, d_a, 2, HEAVY['inn1'])
-    out0, gate0, inn0 = grads(0, 2, d_b, 3, HEAVY['out0']), grads(0, 0, d_a, 0, HEAVY['gate0']), grads(0, 1, d_b, 1, HEAVY['inn0'])
+    outs = gg, gi, go
+
+    def grads(b, m, part, own, ring):
+        name = ('gate', 'in', 'out')[m] + str(b)
+        kit = mine.at[own], held1.at[ring], held2.at[own], sum2.at[own]
+        return Grads(place, Block(place, b, HEAVY[name]), m, part, kit, outs[m], place.slots(17), place.local_slots(1))
+    out1, gate1, inn1 = grads(1, 2, d_a, 0, 0), grads(1, 0, d_b, 1, 1), grads(1, 1, d_a, 2, 2)
+    out0, gate0, inn0 = grads(0, 2, d_b, 3, 3), grads(0, 0, d_a, 4, 0), grads(0, 1, d_b, 0, 1)
     x_copy = place.local(x_in.at[c], xs, place.local_slots(1))
     g_copy = place.local(g_in.at[c], ga.at[:, y], place.local_slots(1))
     save = place.local_slots(8)
@@ -790,57 +792,57 @@
     wait(loads(3))
     hidden_back(n0e, 3, w0o, part, a_s, b_s, 1, dab)
     out1.turn()
+    place.signal(phase.at[1])
     weight_grad_of(n1, dab, 0, d_a)
     out0.combine()
     out0.first.start()
+    place.wait(phase.at[1])
+    gate0.swap()
     back_input(0)
     inn1.first.relay()
     weight_grad_of(n1, dab, GROUPS, d_b)
+    gate0.combine()
+    gate0.first.start()
     out1.second.relay()
     back_input(1)
     d0(0).relay()
+    gate1.turn()
+    out1.last()
+    out1.done()
+    place.signal(phase.at[2])
     out0.first.relay()
-    out1.last()
-    gate1.turn()
     back_input(2)
+    place.wait(phase.at[2])
+    inn0.swap()
     d0(1).relay()
-    out1.done()
-    place.signal(phase.at[1])
+    gate1.second.relay()
+    inn0.combine()
+    inn0.first.start()
     back_input(3)
-    gate1.second.relay()
+    inn1.turn()
     d0(2).relay()
-    place.wait(phase.at[1])
-    gate0.swap()
-    inn1.turn()
-    gate0.combine()
-    gate0.first.start()
+    gate0.first.relay()
+    out0.turn()
     gate1.last()
-    out0.turn()
-    gate1.done()
-    place.signal(phase.at[2])
     inn1.second.relay()
     close_0(0)
     d0(3).relay()
-    place.wait(phase.at[2])
-    inn0.swap()
-    gate0.first.relay()
+    inn0.first.relay()
     out0.second.relay()
-    inn0.combine()
-    inn0.first.start()
+    gate0.turn()
     inn1.last()
     close_0(1)
-    gate0.turn()
-    inn0.first.relay()
     close_0(2)
+    gate0.second.relay()
     out0.last()
     close_0(3)
     dx_slot, dx_local = place.slots(1), place.local_slots(1)
     dx_away, dx_here = place.remote(hs, dx_out.at[c], place.partner, dx_slot), place.local(hs, dx_out.at[c], dx_local)
     dx_away.start()
     dx_here.start()
-    gate0.second.relay()
     inn0.turn()
     gate0.last()
+    gate1.done()
     inn1.done()
     inn0.second.relay()
     inn0.last()
@@ -879,10 +881,10 @@
     + [pltpu.VMEM(WEIGHT, BF16)] * 6
     + [pltpu.VMEM(WEIGHT, F32)] * 2
     + [
-        pltpu.VMEM((4, 4, 4, 2, 16, WIDE), F32),
+        pltpu.VMEM((5, 4, 4, 2, 16, WIDE), F32),
         pltpu.VMEM((4, 3, 2, 2, 2, 16, WIDE), F32),
-        pltpu.VMEM((4, 3, 2, 16, WIDE), F32),
-        pltpu.VMEM((4, 2, 16, WIDE), F32),
+        pltpu.VMEM((5, 3, 2, 16, WIDE), F32),
+        pltpu.VMEM((5, 2, 16, WIDE), F32),
     ]
     + [pltpu.SemaphoreType.DMA((N_REMOTE,)), pltpu.SemaphoreType.DMA((N_REMOTE,)), pltpu.SemaphoreType.DMA((N_LOCAL,))]
     + [pltpu.SemaphoreType.REGULAR((3,))]

time: 241 us -> 228 us (0.946)
  Pallas kernels: 233 us -> 221 us
    pallas_call x1, Pallas kernels: 233 us -> 221 us  [call(): pl.pallas_call(kernel, out_shape=OUTS, in_specs=[ANY] * 2 + [VM] * 3, out...]
where the time goes in v5:
time: 228 us
  Pallas kernels  221 us (97%)
  local copies, waits for them, and re-layouts  6.37 us (3%)
    pallas_call x1, Pallas kernels, call(): pl.pallas_call(kernel, out_shape=OUTS, in_specs=[ANY] * 2 + [VM] * 3, out...  221 us
    unnamed x6, local copies, waits for them, and re-layouts  6.37 us

profile of v5, /device:TPU:0, one launch (start us, length us, event | category | flops | bytes accessed | tf_op | source)
XLA Modules:
  0.0 228.0 jit_solution(5359063549700607254)
XLA Ops:
  0.6 221.0 %kernel_all.1 = (bf16[2,4,2,32,1024]{4,3,2,1,0:T(8,128)(2,1)}, f32[16,4096]{1,0:T(8,128)}, f32[16,4096]{1,0:T(8,128)}, f32[4,16,1024]{2,1,0:T(8,128)}, f32[4,256...) custom-call(bf16[2,4,2,32,1024]{4,3,2,1,0:T(8,128)(2,1)} %bitcast.9,, ...), custom_call_target="tpu_custom_call" | custom-call | tf_op jit(solution)/shard_map/kernel_all/pallas_call | solution.py:895
  221.6 0.0 copy-start
  221.6 2.3 %copy.13 = bf16[8,2,32,1024]{3,2,1,0:T(8,128)(2,1)} copy(bf16[8,2,32,1024]{3,2,1,0:T(8,128)(2,1)} %bitcast.11) | data formatting | bytes 2097152
  223.9 1.7 copy.14
  225.6 1.7 copy.15
  227.3 0.0 copy-done
  227.3 0.7 copy.16
Async XLA Ops:
  221.6 5.7 %copy-start = (f32[4,16,1024]{2,1,0:T(8,128)S(1)}, f32[4,16,1024]{2,1,0:T(8,128)}, u32[]{:S(2)}) copy-start(f32[4,16,1024]{2,1,0:T(8,128)} %get-tuple-element.11) | copy-start | bytes 786436

commit v6 on v5

--- a/solution.py
+++ b/solution.py
@@ -713,12 +713,12 @@
     close_o(0)
     o(1).relay()
     o(2).start()
+    n(0).relay()
+    w1.step5()
     forward(3)
     n_save.wait()
     place.signal(phase.at[0])
     v0.send()
-    n(0).relay()
-    w1.step5()
     o(2).relay()
     o(3).start()
     loop(CHUNKS, lambda k: g(k).finish())

time: 228 us -> 228 us (level)
  no operation moved by 1% of the time
where the time goes in v6:
time: 228 us
  Pallas kernels  221 us (97%)
  local copies, waits for them, and re-layouts  6.37 us (3%)
    pallas_call x1, Pallas kernels, call(): pl.pallas_call(kernel, out_shape=OUTS, in_specs=[ANY] * 2 + [VM] * 3, out...  221 us
    unnamed x6, local copies, waits for them, and re-layouts  6.37 us

profile of v6, /device:TPU:0, one launch (start us, length us, event | category | flops | bytes accessed | tf_op | source)
XLA Modules:
  0.0 228.1 jit_solution(16477394514665438036)
XLA Ops:
  0.6 221.0 %kernel_all.1 = (bf16[2,4,2,32,1024]{4,3,2,1,0:T(8,128)(2,1)}, f32[16,4096]{1,0:T(8,128)}, f32[16,4096]{1,0:T(8,128)}, f32[4,16,1024]{2,1,0:T(8,128)}, f32[4,256...) custom-call(bf16[2,4,2,32,1024]{4,3,2,1,0:T(8,128)(2,1)} %bitcast.9,, ...), custom_call_target="tpu_custom_call" | custom-call | tf_op jit(solution)/shard_map/kernel_all/pallas_call | solution.py:895
  221.7 0.0 copy-start
  221.7 2.3 %copy.13 = bf16[8,2,32,1024]{3,2,1,0:T(8,128)(2,1)} copy(bf16[8,2,32,1024]{3,2,1,0:T(8,128)(2,1)} %bitcast.11) | data formatting | bytes 2097152
  224.0 1.7 copy.14
  225.7 1.7 copy.15
  227.4 0.0 copy-done
  227.4 0.7 copy.16
Async XLA Ops:
  221.7 5.7 %copy-start = (f32[4,16,1024]{2,1,0:T(8,128)S(1)}, f32[4,16,1024]{2,1,0:T(8,128)}, u32[]{:S(2)}) copy-start(f32[4,16,1024]{2,1,0:T(8,128)} %get-tuple-element.11) | copy-start | bytes 786436
